TPU v7x, 512 devices: a whole 4x4x16 slice. The times are simulated.
512 devices in a mesh: tm: 8 (over y_lo, x), band: 64 (over z, y_hi, core).
Axes of the slice: x: 4, y: 4 (y_hi: 2, y_lo: 2; y = y_hi * 2 + y_lo), z: 16, core: 2. Of those that a mesh axis runs over, the one named last changes fastest.
Arguments:
- samples: bfloat16 [2048, 256, 2, 512], P('tm', 'band'), may hold values from -6 to 6
- weights: bfloat16 [256, 2, 512, 512], P('band', None, None, 'tm'), may hold values from -0.25 to 0.25
- prototype: float32 [1024], replicated, may hold values from 0.25 to 1
Outputs:
- beam_series: float32 [512, 524288], P('band', 'tm')
All inputs are finite; a program needn't handle non-finite values.
Results may differ from a plain program's by a relative error of at most 0.004.
Values may be sent and summed in bfloat16 or wider, within the bound.
No kernel may reach another device: no remote copies, remote signals or barrier semaphores. Data moves between devices by JAX's collectives and lax.ppermute only.
A program may use at most 128 MiB of HBM per device.

v0:
```python
import math

import jax
import jax.numpy as jnp
from jax import lax
from jax.sharding import PartitionSpec as P

M = 512
K = 256
FIRST_BIN = 32


def passed_along(block, axis, distance):
    devices = range(lax.axis_size(axis))
    route = [(i - distance, i) for i in devices if i - distance in devices]
    return lax.ppermute(block, axis, route)


def synth_table(prototype):
    length = prototype.shape[0]
    bin_index = jnp.arange(K, dtype=jnp.int32) + FIRST_BIN
    tap_index = jnp.arange(length, dtype=jnp.int32)
    phase_index = bin_index[:, None] * tap_index[None, :] % M
    angles = phase_index.astype(jnp.float32) * (2.0 * math.pi / M)
    scaled = prototype[None, :] / math.sqrt(K)
    window_table = jnp.stack([jnp.cos(angles) * scaled, -jnp.sin(angles) * scaled], axis=1)
    return window_table.astype(jnp.bfloat16)


def intersection_add(frames, hop_size):
    pieces = frames.shape[-1] // hop_size
    pieces_view = frames.reshape(frames.shape[:-1] + (pieces, hop_size))
    leading = [(0, 0)] * (pieces_view.ndim - 3)
    intersection = jnp.zeros(
        pieces_view.shape[:-3] + (pieces_view.shape[-3] + pieces - 1, hop_size), frames.dtype
    )
    for lag in range(pieces):
        intersection = intersection + jnp.pad(
            pieces_view[..., lag, :], leading + [(lag, pieces - 1 - lag), (0, 0)]
        )
    return intersection


def beam_form(samples, weights):
    products = jnp.einsum("fkce,kdeb->bkdcf", samples, weights, preferred_element_type=jnp.float32)
    real_part = products[:, :, 0, 0] + products[:, :, 1, 1]
    imag_part = products[:, :, 0, 1] - products[:, :, 1, 0]
    return jnp.stack([real_part, imag_part], axis=2).astype(jnp.bfloat16)


def synthesize(spectra, window_table):
    return jnp.einsum("bkcf,kcn->bfn", spectra, window_table, preferred_element_type=jnp.float32)


def shards(samples, weights, prototype):
    hop_size = M // 2
    beam_parts = beam_form(samples, lax.all_gather(weights, "tm", axis=3, tiled=True))
    gathered = lax.all_to_all(beam_parts, "band", split_axis=0, concat_axis=1, tiled=True)
    window_table = synth_table(prototype)
    frame_total = gathered.shape[3]
    tail_rows = prototype.shape[0] // hop_size - 1
    frames = synthesize(gathered, window_table)
    summed = intersection_add(frames, hop_size)
    prev_tail = passed_along(summed[:, frame_total:], "tm", 1)
    block_out = summed[:, :frame_total]
    block_out = jnp.concatenate(
        [block_out[:, :tail_rows] + prev_tail, block_out[:, tail_rows:]], axis=1
    )
    return block_out.reshape(block_out.shape[0], frame_total * hop_size)


def solution(mesh):
    in_specs = (P("tm", "band", None, None), P("band", None, None, "tm"), P())
    out_specs = P("band", "tm")
    return jax.shard_map(shards, mesh=mesh, in_specs=in_specs, out_specs=out_specs, check_vma=False)
```

profile of v0, /device:TPU:24, one launch (start us, length us, event | category | flops | bytes accessed | tf_op | source)
XLA Modules:
  0.0 223.1 jit_solution(4753085409509677167)
XLA Ops:
  6.5 0.0 copy-start
  6.5 0.0 all-gather.2.cloned.1.call-start
  6.5 0.7 all-gather.2.cloned.1.call-update
  7.3 65.9 %all-gather.2.cloned.1.call-done = bf16[4,2,512,512]{2,3,1,0:T(8,128)(2,1)} async-done(((bf16[4,2,512,64]{2,3,1,0:T(8,128)(2,1)}), bf16[4,2,512,512]{2,3,1,0:T(8,128)(2,1)}) %all-gather.2.cloned.1.call-update) | async-done | bytes 4194320 | tf_op jit(solution)/shard_map/all_gather | solution.py:57
  73.2 0.0 copy-done
  73.2 4.6 %fusion.2 = f32[512,4,2,2,256]{4,0,3,2,1:T(8,128)S(1)} fusion(bf16[4,2,512,512]{2,3,1,0:T(8,128)(2,1)} %all-gather.2.cloned.1.call-done, bf16[256,4,2,512,1]{3,2,1,0,4:T(2,128)(2,1)S(1)} %bitcast.62), kind=kOutput, calls=%fused_computation.2 | convolution fusion | flops 2147483648 | bytes 14680064 | tf_op jit(solution)/shard_map/fkce,kdeb->bkdcf/dot_general | solution.py:45
  77.8 0.4 fusion.14
  78.1 0.2 fusion.13
  78.4 0.2 pad_maximum_fusion
  78.6 2.9 %copy.32 = bf16[512,4,2,256]{3,1,2,0:T(4,128)(2,1)} copy(bf16[512,4,2,256]{3,0,1,2:T(8,128)(2,1)S(1)} %pad_maximum_fusion) | data formatting | bytes 4194304 | tf_op jit(solution)/shard_map/stack | solution.py:48
  81.5 0.0 copy-start.1
  81.5 16.0 %all-to-all-start = ((bf16[512,4,2,256]{3,1,2,0:T(4,128)(2,1)}), bf16[512,4,2,256]{3,1,2,0:T(4,128)(2,1)}, u32[]{:S(2)}, u32[]{:S(2)}) async-start(bf16[512,4,2,256]{3,1,2,0:T(4,128)(2,1)} %copy.32), calls=%async_computation | async-start | bytes 4194304 | tf_op jit(solution)/shard_map/all_to_all | solution.py:58
  97.6 0.0 copy-done.1
  97.6 4.6 %multiply_convert_fusion.1 = (bf16[256,1,1024]{0,2,1:T(8,128)(2,1)S(1)}, bf16[256,1,1024]{0,2,1:T(8,128)(2,1)S(1)}) fusion(f32[1024]{0:T(1024)S(1)} %broadcast_multiply_fusion, s32[256]{0:T(256)S(1)} %iota_add_fusion), kind=kLoop, calls=%fused_computation.34 | loop fusion | flops 4980736 | bytes 1053696 | tf_op jit(solution)/shard_map/convert
  102.2 0.1 pad_maximum_fusion.1
  102.3 96.1 %all-to-all-done = bf16[512,4,2,256]{3,1,2,0:T(4,128)(2,1)} async-done(((bf16[512,4,2,256]{3,1,2,0:T(4,128)(2,1)}), bf16[512,4,2,256]{3,1,2,0:T(4,128)(2,1)}, u32[]{:S(2)}, u32[]{:S(2)}) %all-to-all-start) | async-done | bytes 2097184 | tf_op jit(solution)/shard_map/all_to_all | solution.py:58
  198.4 2.0 copy.63
  200.5 0.3 copy.34
  200.7 3.9 %convolution_bitcast_fusion = f32[8,256,4,256]{3,1,2,0:T(8,128)S(1)} fusion(bf16[8,256,2,256,1]{3,0,2,1,4:T(8,128)(2,1)S(1)} %bitcast.64, bf16[4,256,2,256]{3,1,0,2:T(8,128)(2,1)S(1)} %bitcast.65), kind=kOutput, calls=%fused_computation.3 | convolution fusion | flops 2147483648 | bytes 11534336 | tf_op jit(solution)/shard_map/bkcf,kcn->bfn/dot_general | solution.py:52
  204.7 0.9 slice_bitcast_fusion.3
  205.6 1.9 collective-permute-start
  207.5 0.6 pad_add_fusion
  208.1 5.4 %collective-permute-done = f32[8,3,256]{2,1,0:T(4,128)S(1)} collective-permute-done((f32[8,3,256]{2,1,0:T(4,128)S(1)}, f32[8,3,256]{2,1,0:T(4,128)S(1)}, u32[]{:S(2)}, u32[]{:S(2)}) %collective-permute-start) | collective-permute-done | bytes 24608 | tf_op jit(solution)/shard_map/ppermute | solution.py:16
  213.5 0.2 maximum_bitcast_fusion
  213.7 2.5 %copy.53 = f32[1,8,256,256]{3,1,2,0:T(8,128)} copy(f32[1,8,256,256]{3,2,1,0:T(8,128)S(1)} %maximum_bitcast_fusion) | data formatting | bytes 4194304
  (4 shorter events, 0.1 us)
Async XLA Ops:
  6.5 66.6 %copy-start = (bf16[256,4,2,512]{3,2,1,0:T(2,128)(2,1)S(1)}, bf16[256,4,2,512]{3,2,1,0:T(2,128)(2,1)}, u32[]{:S(2)}) copy-start(bf16[256,4,2,512]{3,2,1,0:T(2,128)(2,1)} %param.3) | copy-start | bytes 6291460
  6.5 66.6 %all-gather.2.cloned.1.call-start = ((), (), s32[]{:S(2)}) async-start(), calls=%async_computation.1 | async-start | bytes 4718592 | tf_op jit(solution)/shard_map/all_gather | solution.py:57
  81.5 16.0 %copy-start.1 = (f32[1024]{0:T(1024)S(1)}, f32[1024]{0:T(1024)}, u32[]{:S(2)}) copy-start(f32[1024]{0:T(1024)} %param.5) | copy-start | bytes 12292
  81.5 116.9 %all-to-all-start = ((bf16[512,4,2,256]{3,1,2,0:T(4,128)(2,1)}), bf16[512,4,2,256]{3,1,2,0:T(4,128)(2,1)}, u32[]{:S(2)}, u32[]{:S(2)}) async-start(bf16[512,4,2,256]{3,1,2,0:T(4,128)(2,1)} %copy.32), calls=%async_computation | async-start | bytes 4194304 | tf_op jit(solution)/shard_map/all_to_all | solution.py:58
  205.6 7.9 %collective-permute-start = (f32[8,3,256]{2,1,0:T(4,128)S(1)}, f32[8,3,256]{2,1,0:T(4,128)S(1)}, u32[]{:S(2)}, u32[]{:S(2)}) collective-permute-start(f32[8,3,256]{2,1,0:T(4,128)S(1)} %pad_add_fusion.3), channel_id=1, source_target_pairs={{0,64},{64,128},{128,192},{192,256},{256,320},{320,384},{384,448},... | collective-permute-start | bytes 73736 | tf_op jit(solution)/shard_map/ppermute | solution.py:16
Sparse Core Ops, SparseCore 0:
  9.4 63.7 all-gather.1
where the time goes:
time: 223 us
  waiting for transfers between devices  168 us (75%)
  starting transfers between devices  17.9 us (8%)
  between operations  13.5 us (6%)
  local copies, waits for them, and re-layouts  8.63 us (4%)
  matrix products  8.48 us (4%)
  other arithmetic  6.42 us (3%)
    all_to_all x1, waiting for transfers between devices, shards(): lax.all_to_all(beam_parts, 'band', split_axis=0, concat_axis=1, tiled=True)  96.1 us
    all_gather x1, waiting for transfers between devices, shards(): lax.all_gather(weights, 'tm', axis=3, tiled=True)  65.9 us
    all_to_all x1, starting transfers between devices, shards(): lax.all_to_all(beam_parts, 'band', split_axis=0, concat_axis=1, tiled=True)  16 us
    ppermute x1, waiting for transfers between devices, passed_along(): return lax.ppermute(block, axis, route)  5.36 us
    another operation x1, other arithmetic  4.64 us
    dot_general x1, matrix products, beam_form(): jnp.einsum('fkce,kdeb->bkdcf', samples, weights, preferred_element_type=j...  4.57 us
  transfers between devices with their start and end apart: 3, of which 3 were waited for; matrix products, arithmetic and copies ran while one was open for 2% of the time, Pallas kernels for 0%

commit v1 on v0

v1 whole, which is shorter than its diff:
```python
import math

import jax
import jax.numpy as jnp
from jax import lax
from jax.experimental import pallas as pl
from jax.experimental.pallas import tpu as pltpu
from jax.sharding import PartitionSpec as P


M = 512
K = 256
FIRST_BIN = 32
LANES = 128
HEAD = 1


def passed_along(block, axis, distance):
    devices = range(lax.axis_size(axis))
    route = [(i - distance, i) for i in devices if i - distance in devices]
    return lax.ppermute(block, axis, route)


def synth_table(prototype):
    length = prototype.shape[0]
    bin_index = jnp.arange(K, dtype=jnp.int32) + FIRST_BIN
    tap_index = jnp.arange(length, dtype=jnp.int32)
    phase_index = bin_index[:, None] * tap_index[None, :] % M
    angles = phase_index.astype(jnp.float32) * (2.0 * math.pi / M)
    scaled = prototype[None, :] / math.sqrt(K)
    window_table = jnp.stack([jnp.cos(angles) * scaled, -jnp.sin(angles) * scaled], axis=1)
    return window_table.astype(jnp.bfloat16)


def intersection_add(frames, hop_size):
    pieces = frames.shape[-1] // hop_size
    pieces_view = frames.reshape(frames.shape[:-1] + (pieces, hop_size))
    leading = [(0, 0)] * (pieces_view.ndim - 3)
    intersection = jnp.zeros(
        pieces_view.shape[:-3] + (pieces_view.shape[-3] + pieces - 1, hop_size), frames.dtype
    )
    for lag in range(pieces):
        intersection = intersection + jnp.pad(
            pieces_view[..., lag, :], leading + [(lag, pieces - 1 - lag), (0, 0)]
        )
    return intersection


def overlap_kernel(frames_ref, base_ref, out_ref):
    beams, rows, hop_size = base_ref.shape
    lags = frames_ref.shape[2] // hop_size
    step, lanes = 32, out_ref.shape[1]
    halves = hop_size // lanes

    def one_beam(b, carry):
        for at in range(0, rows, step):
            total = base_ref[b, pl.ds(at, step), :] + frames_ref[b, pl.ds(at, step), :hop_size]
            for lag in range(1, lags):
                columns = pl.ds(lag * hop_size, hop_size)
                if at:
                    total += frames_ref[b, pl.ds(at - lag, step), columns]
                else:
                    piece = pltpu.roll(frames_ref[b, pl.ds(0, step), columns], lag, 0)
                    row = lax.broadcasted_iota(jnp.int32, piece.shape, 0)
                    total += jnp.where(row < lag, 0.0, piece)
            for half in range(halves):
                rows_of = pl.ds((at * halves + half) * beams + b, step, stride=halves * beams)
                out_ref[rows_of, :] = total[:, half * lanes : (half + 1) * lanes]
        return carry

    lax.fori_loop(0, beams, one_beam, 0)


def overlapped(frames, base):
    beams, rows, hop_size = base.shape
    lags = frames.shape[2] // hop_size
    whole = pl.BlockSpec(memory_space=pltpu.VMEM)
    return pl.pallas_call(
        overlap_kernel,
        out_shape=jax.ShapeDtypeStruct((rows * hop_size // LANES * beams, LANES), jnp.float32),
        in_specs=[whole, whole],
        out_specs=whole,
        cost_estimate=pl.CostEstimate(
            flops=beams * lags * rows * hop_size,
            bytes_accessed=4 * beams * (lags + 2) * rows * hop_size,
            transcendentals=0,
        ),
        compiler_params=pltpu.CompilerParams(vmem_limit_bytes=20 * 2**20),
        name="overlap",
    )(frames, base)


def exchanged(block, axis):
    return lax.all_to_all(block, axis, split_axis=0, concat_axis=0, tiled=True)


def gathered_by_permutes(block):
    size = lax.axis_size("tm")
    ring = size // 2

    def moved(array, x_step, y_step):
        route = [
            (i, ((i // ring + y_step) % 2) * ring + (i % ring + x_step) % ring)
            for i in range(size)
        ]
        return lax.ppermute(array, "tm", route)

    half = block.shape[-2] // 2
    left = moved(block, 1, 0)
    right = moved(block, -1, 0)
    across = moved(block, 0, 1)
    far_a = moved(left[..., :half, :], 1, 0)
    far_b = moved(right[..., half:, :], -1, 0)
    across_left = moved(across, 1, 0)
    across_right = moved(across, -1, 0)
    across_far = moved(block, 2, 1)
    far = jnp.concatenate([far_a, far_b], axis=-2)
    me = lax.axis_index("tm")
    y, x = me // ring, me % ring
    table = jnp.zeros((size,) + block.shape, block.dtype)
    for piece, dx, dy in (
        (block, 0, 0), (left, -1, 0), (right, 1, 0), (far, 2, 0),
        (across, 0, 1), (across_left, -1, 1), (across_right, 1, 1), (across_far, 2, 1),
    ):
        at = ((y + dy) % 2) * ring + (x + dx + ring) % ring
        table = lax.dynamic_update_slice(table, piece[None], (at,) + (0,) * block.ndim)
    return table


def beam_form(samples, weights):
    products = jnp.einsum(
        "pfkce,tkcbe->tbkpf", samples, weights, preferred_element_type=jnp.float32
    )
    spectra = products.astype(jnp.bfloat16)
    size = lax.axis_size("band")
    spectra = spectra.reshape((size, -1) + spectra.shape[2:])
    return jnp.transpose(spectra, (0, 2, 3, 1, 4))


def shards(samples, weights, prototype):
    hop_size = M // 2
    blocks = jnp.transpose(weights, (0, 1, 3, 2))
    size = lax.axis_size("tm")
    head = blocks[:HEAD]
    head = exchanged(jnp.broadcast_to(head[None], (size,) + head.shape), "tm")
    both = jnp.stack([samples, jnp.stack([samples[:, :, 1], -samples[:, :, 0]], axis=2)])
    head_spectra = exchanged(beam_form(both[:, :, :HEAD], head), "band")
    rest = gathered_by_permutes(blocks[HEAD:])
    rest_spectra = exchanged(beam_form(both[:, :, HEAD:], rest), "band")

    table = synth_table(prototype)
    table = table.reshape((lax.axis_size("band"), -1) + table.shape[1:])

    frame_total = samples.shape[0]
    beams = head_spectra.shape[3]
    lags = prototype.shape[0] // hop_size

    def synthesize(spectra, part):
        return jnp.einsum(
            "skcbf,skcm->bfm", spectra, part, preferred_element_type=jnp.float32
        )

    def spill_of(tail):
        tail = tail.reshape(beams, lags - 1, lags, hop_size)
        rows = []
        for row in range(lags - 1):
            rows.append(
                sum(tail[:, lags - 1 + row - lag, lag] for lag in range(row + 1, lags))
            )
        return jnp.stack(rows)

    base = intersection_add(synthesize(head_spectra, table[:, :HEAD]), hop_size)
    base, spill = base[:, :frame_total], base[:, frame_total:]
    base, spill, rest_spectra = lax.optimization_barrier((base, spill, rest_spectra))
    rest_frames = synthesize(rest_spectra, table[:, HEAD:])
    spill = spill_of(rest_frames[:, frame_total - lags + 1 :]) + jnp.transpose(spill, (1, 0, 2))
    spill = spill.reshape(lags - 1, beams, -1, LANES)
    spill = jnp.transpose(spill, (0, 2, 1, 3)).reshape(-1, LANES)
    prev_tail = passed_along(spill, "tm", 1)
    out = overlapped(rest_frames, base)
    out = lax.dynamic_update_slice(out, out[: prev_tail.shape[0]] + prev_tail, (0, 0))
    out = out.reshape(-1, beams, LANES)
    return jnp.transpose(out, (1, 0, 2)).reshape(beams, frame_total * hop_size)


def solution(mesh):
    in_specs = (P("tm", "band", None, None), P("band", None, None, "tm"), P())
    out_specs = P("band", "tm")

    return jax.shard_map(shards, mesh=mesh, in_specs=in_specs, out_specs=out_specs, check_vma=False)
```

time: 223 us -> 199 us (0.89)
  waiting for transfers between devices: 168 us -> 91.9 us
  starting transfers between devices: 17.9 us -> 58.7 us
  local copies, waits for them, and re-layouts: 8.63 us -> 22.8 us
  between operations: 13.5 us -> 0.45 us
  other arithmetic: 6.42 us -> 10.3 us
  Pallas kernels: 0 us -> 2.64 us
  matrix products: 8.48 us -> 11.1 us
    all_gather x1 -> x0, waiting for transfers between devices: 65.9 us -> none  [shards(): lax.all_gather(weights, 'tm', axis=3, tiled=True)]
    ppermute x0 -> x8, starting transfers between devices: none -> 26.9 us  [moved(): return lax.ppermute(array, 'tm', route)]
    all_to_all x1 -> x3, starting transfers between devices: 16 us -> 29.9 us  [exchanged(): return lax.all_to_all(block, axis, split_axis=0, concat_axis=0, tiled=True)]
    dynamic_update_slice x0 -> x7, local copies, waits for them, and re-layouts: none -> 9.48 us  [gathered_by_permutes(): lax.dynamic_update_slice(table, piece[None], (at,) + (0,) * block.ndim)]
    all_to_all x1 -> x3, waiting for transfers between devices: 96.1 us -> 87.5 us  [exchanged(): return lax.all_to_all(block, axis, split_axis=0, concat_axis=0, tiled=True)]
    broadcast_in_dim x0 -> x3, local copies, waits for them, and re-layouts: none -> 4.08 us  [the longest x2 2.07 us: shards(): head = exchanged(jnp.broadcast_to(head[None], (size,) + head.shape), 'tm')]
    dynamic_update_slice x0 -> x2, other arithmetic: none -> 3.3 us  [the longest x1 1.95 us: gathered_by_permutes(): lax.dynamic_update_slice(table, piece[None], (at,) + (0,) * block.ndim)]
    another operation x1 -> x0, local copies, waits for them, and re-layouts: 2.94 us -> none  [beam_form(): return jnp.stack([real_part, imag_part], axis=2).astype(jnp.bfloat16)]
  transfers between devices with their start and end apart: 3 -> 12, of which waited for: 3 -> 4; matrix products, arithmetic and copies ran while one was open for 2% -> 18% of each run, Pallas kernels for 0% -> 1%
where the time goes in v1:
time: 199 us; the launch traced here: 198 us
  waiting for transfers between devices  91.9 us (46%)
  starting transfers between devices  58.7 us (29%)
  local copies, waits for them, and re-layouts  22.8 us (11%)
  matrix products  11.1 us (6%)
  other arithmetic  10.3 us (5%)
  Pallas kernels  2.64 us (1%)
    all_to_all x3, waiting for transfers between devices, exchanged(): return lax.all_to_all(block, axis, split_axis=0, concat_axis=0, tiled=True)  87.5 us
    all_to_all x3, starting transfers between devices, exchanged(): return lax.all_to_all(block, axis, split_axis=0, concat_axis=0, tiled=True)  29.9 us
    ppermute x8, starting transfers between devices, moved(): return lax.ppermute(array, 'tm', route)  26.9 us
    dynamic_update_slice x7, local copies, waits for them, and re-layouts, gathered_by_permutes(): lax.dynamic_update_slice(table, piece[None], (at,) + (0,) * block.ndim)  9.48 us
    dot_general x2, matrix products, beam_form(): jnp.einsum('pfkce,tkcbe->tbkpf', samples, weights, preferred_element_type...  5.84 us
    dot_general x2, matrix products, synthesize(): jnp.einsum('skcbf,skcm->bfm', spectra, part, preferred_element_type=jnp.f...  5.22 us
    another operation x1, other arithmetic  4.59 us
  transfers between devices with their start and end apart: 12, of which 4 were waited for; matrix products, arithmetic and copies ran while one was open for 18% of the time, Pallas kernels for 1%

profile of v1, /device:TPU:24, one launch (start us, length us, event | category | flops | bytes accessed | tf_op | source)
XLA Modules:
  0.0 197.9 jit_solution(3369615688109450706)
XLA Ops:
  2.1 5.8 %all-to-all-start = ((bf16[8,1,2,64,512]{4,3,2,1,0:T(8,128)(2,1)}), bf16[8,1,2,64,512]{4,3,2,1,0:T(8,128)(2,1)}, u32[]{:S(2)}, u32[]{:S(2)}) async-start(bf16[8,1,2,64,512]{4,3,2,1,0:T(8,128)(2,1)} %broadcast_in_dim.39), calls=%async_computation | async-start | bytes 2097152 | tf_op jit(solution)/shard_map/all_to_all | solution.py:94
  8.6 1.9 collective-permute-start.4
  10.5 5.1 %collective-permute-start.1 = (bf16[3,2,64,512]{3,2,1,0:T(8,128)(2,1)}, bf16[3,2,64,512]{3,2,1,0:T(8,128)(2,1)S(1)}, u32[]{:S(2)}, u32[]{:S(2)}) collective-permute-start(bf16[3,2,64,512]{3,2,1,0:T(8,128)(2,1)} %slice.104), channel_id=1, source_target_pairs={{0,192},{64,0},{128,64},{192,128},{256,448},{320,256},{384,320},{4... | collective-permute-start | bytes 1179656 | tf_op jit(solution)/shard_map/ppermute | solution.py:106
  15.7 1.9 collective-permute-start
  17.6 5.1 %collective-permute-start.7 = (bf16[3,2,64,512]{3,2,1,0:T(8,128)(2,1)}, bf16[3,2,64,512]{3,2,1,0:T(8,128)(2,1)}, u32[]{:S(2)}, u32[]{:S(2)}) collective-permute-start(bf16[3,2,64,512]{3,2,1,0:T(8,128)(2,1)} %slice.104), channel_id=1, source_target_pairs={{0,384},{64,448},{128,256},{192,320},{256,128},{320,192},{384,0},{... | collective-permute-start | bytes 1179656 | tf_op jit(solution)/shard_map/ppermute | solution.py:106
  22.9 2.3 %copy.89 = bf16[256,4,2,512]{3,0,2,1:T(8,128)(2,1)S(1)} copy(bf16[256,4,2,512]{3,2,1,0:T(2,128)(2,1)} %param.3) | data formatting | bytes 4194304 | tf_op args[0]
  25.3 1.5 maximum_bitcast_fusion
  26.8 2.0 %broadcast_in_dim.40 = bf16[8,3,2,64,512]{4,3,2,0,1:T(8,128)(2,1)} broadcast(bf16[]{:T(256)} %constant.106.clone.1), dimensions={} | broadcast | bytes 3145730 | tf_op jit(solution)/shard_map/broadcast_in_dim | solution.py:120
  31.4 3.8 %collective-permute-start.3 = (bf16[3,2,32,512]{3,2,1,0:T(8,128)(2,1)}, bf16[3,2,32,512]{3,2,1,0:T(8,128)(2,1)}, u32[]{:S(2)}, u32[]{:S(2)}) collective-permute-start(bf16[3,2,32,512]{3,2,1,0:T(8,128)(2,1)} %slice.106), channel_id=1, source_target_pairs={{0,192},{64,0},{128,64},{192,128},{256,448},{320,256},{384,320},{4... | collective-permute-start | bytes 589832 | tf_op jit(solution)/shard_map/ppermute | solution.py:106
  36.0 2.0 %collective-permute-start.2 = (bf16[3,2,32,512]{3,2,1,0:T(8,128)(2,1)}, bf16[3,2,32,512]{3,2,1,0:T(8,128)(2,1)}, u32[]{:S(2)}, u32[]{:S(2)}) collective-permute-start(bf16[3,2,32,512]{3,2,1,0:T(8,128)(2,1)} %slice.105), channel_id=1, source_target_pairs={{0,64},{64,128},{128,192},{192,0},{256,320},{320,384},{384,448},{4... | collective-permute-start | bytes 589832 | tf_op jit(solution)/shard_map/ppermute | solution.py:106
  38.0 5.0 %collective-permute-start.6 = (bf16[3,2,64,512]{3,2,1,0:T(8,128)(2,1)}, bf16[3,2,64,512]{3,2,1,0:T(8,128)(2,1)}, u32[]{:S(2)}, u32[]{:S(2)}) collective-permute-start(bf16[3,2,64,512]{3,2,1,0:T(8,128)(2,1)} %collective-permute-done.4), channel_id=1, source_target_pairs={{0,192},{64,0},{128,64},{192,128},{256,448},{320,256},{384,320},{4... | collective-permute-start | bytes 1179656 | tf_op jit(solution)/shard_map/ppermute | solution.py:106
  43.1 1.9 collective-permute-start.5
  45.0 2.1 %fusion.15 = bf16[2,256,8,64]{1,3,2,0:T(8,128)(2,1)S(1)} fusion(bf16[1,256,4,2,512]{4,1,3,0,2:T(8,128)(2,1)} %maximum_bitcast_fusion, bf16[1,256,4,2,512]{4,1,3,0,2:T(8,128)(2,1)S(1)} %bitcast.142, bf16[8,1,2,64,512]{4,3,2,1,0:T(8,128)(2,1)} %all-to-all-done), kind=kOutput, calls=%fused_computation.20 | convolution fusion | flops 539230208 | bytes 5767168 | tf_op jit(solution)/shard_map/pfkce,tkcbe->tbkpf/dot_general | solution.py:131
  47.1 1.3 copy.88
  48.5 18.6 %all-to-all-start.1 = ((bf16[64,1,2,8,256]{4,2,3,1,0:T(2,128)(2,1)}), bf16[64,1,2,8,256]{4,2,3,1,0:T(2,128)(2,1)S(1)}, u32[]{:S(2)}, u32[]{:S(2)}) async-start(bf16[64,1,2,8,256]{4,2,3,1,0:T(2,128)(2,1)} %bitcast.140), calls=%async_computation.1 | async-start | bytes 1048576 | tf_op jit(solution)/shard_map/all_to_all | solution.py:94
  68.6 2.0 fusion.30
  70.6 1.8 bitcast_dynamic-update-slice_fusion.3
  72.4 1.8 bitcast_dynamic-update-slice_fusion.2
  74.2 1.8 bitcast_dynamic-update-slice_fusion.1
  76.0 1.8 bitcast_dynamic-update-slice_fusion
  77.7 3.7 %fusion.10 = bf16[8,64,3,2,256]{4,1,3,0,2:T(8,128)(2,1)S(1)} fusion(bf16[1,256,4,2,512]{4,1,3,0,2:T(8,128)(2,1)S(1)} %copy-done, bf16[1,256,4,2,512]{4,1,3,0,2:T(8,128)(2,1)S(1)} %bitcast.143, bf16[8,3,2,64,512]{4,3,2,0,1:T(8,128)(2,1)} %bitcast_dynamic-update-slice_fusion), kind=kOutput, calls=%fused_computation.18 | convolution fusion | flops 1617690624 | bytes 8912896 | tf_op jit(solution)/shard_map/pfkce,tkcbe->tbkpf/dot_general | solution.py:131
  81.6 1.3 copy.60
  82.8 17.8 %all-to-all-done.1 = bf16[64,1,2,8,256]{4,2,3,1,0:T(2,128)(2,1)S(1)} async-done(((bf16[64,1,2,8,256]{4,2,3,1,0:T(2,128)(2,1)}), bf16[64,1,2,8,256]{4,2,3,1,0:T(2,128)(2,1)S(1)}, u32[]{:S(2)}, u32[]{:S(2)}) %all-to-all-start.1) | async-done | bytes 524320 | tf_op jit(solution)/shard_map/all_to_all | solution.py:94
  100.6 5.5 %all-to-all-start.2 = ((bf16[64,3,2,8,256]{4,3,2,1,0:T(8,128)(2,1)}), bf16[64,3,2,8,256]{4,3,2,1,0:T(8,128)(2,1)}, u32[]{:S(2)}, u32[]{:S(2)}) async-start(bf16[64,3,2,8,256]{4,3,2,1,0:T(8,128)(2,1)} %copy.60), calls=%async_computation.2 | async-start | bytes 3145728 | tf_op jit(solution)/shard_map/all_to_all | solution.py:94
  106.2 4.6 %multiply_convert_fusion.1 = (bf16[64,4,1,1024]{3,0,1,2:T(8,128)(2,1)S(1)}, bf16[64,4,1,1024]{3,0,1,2:T(8,128)(2,1)S(1)}) fusion(f32[1024]{0:T(1024)S(1)} %broadcast_multiply_fusion, s32[64,4]{0,1:T(4,128)S(1)} %add_add_fusion), kind=kLoop, calls=%fused_computation.30 | loop fusion | flops 4980736 | bytes 1053696 | tf_op jit(solution)/shard_map/convert
  111.8 1.3 convolution_bitcast_fusion.1
  114.9 69.7 %all-to-all-done.2 = bf16[64,3,2,8,256]{4,3,2,1,0:T(8,128)(2,1)} async-done(((bf16[64,3,2,8,256]{4,3,2,1,0:T(8,128)(2,1)}), bf16[64,3,2,8,256]{4,3,2,1,0:T(8,128)(2,1)}, u32[]{:S(2)}, u32[]{:S(2)}) %all-to-all-start.2) | async-done | bytes 1572896 | tf_op jit(solution)/shard_map/all_to_all | solution.py:94
  184.6 3.9 %convolution_bitcast_fusion.frames_ref = f32[8,256,1024]{2,1,0:T(8,128)S(1)} fusion(bf16[64,3,2,8,256]{4,3,2,1,0:T(8,128)(2,1)} %all-to-all-done.2, bf16[64,4,1,1024]{3,0,1,2:T(8,128)(2,1)S(1)} %copy-done.2, bf16[64,4,1,1024]{3,0,1,2:T(8,128)(2,1)S(1)} %get-tuple-element.22), kind=kOutput, calls=%fused_computation | convolution fusion | flops 1611005952 | bytes 11010048 | tf_op jit(solution)/shard_map/skcbf,skcm->bfm/dot_general | solution.py:159
  188.7 1.9 collective-permute-start.8
  190.6 2.6 %overlap.1 = f32[4096,128]{1,0:T(8,128)} custom-call(f32[8,256,1024]{2,1,0:T(8,128)S(1)} %convolution_bitcast_fusion.frames_ref, f32[8,256,256]{2,1,0:T(8,128)S(1)} %slice.103.base_ref), custom_call_target="tpu_custom_call" | custom-call | flops 2097152 | bytes 12582912 | tf_op jit(solution)/shard_map/overlap/pallas_call | solution.py:78
  193.3 3.3 %collective-permute-done.8 = f32[48,128]{1,0:T(8,128)S(1)} collective-permute-done((f32[48,128]{1,0:T(8,128)S(1)}, f32[48,128]{1,0:T(8,128)S(1)}, u32[]{:S(2)}, u32[]{:S(2)}) %collective-permute-start.8) | collective-permute-done | bytes 24608 | tf_op jit(solution)/shard_map/ppermute | solution.py:21
  196.5 1.4 fusion.32
  (41 shorter events, 10.9 us)
Async XLA Ops:
  0.0 7.8 %copy-start.3 = (bf16[4,2,512,64]{2,3,1,0:T(8,128)(2,1)S(1)}, bf16[4,2,512,64]{2,3,1,0:T(8,128)(2,1)}, u32[]{:S(2)}) copy-start(bf16[4,2,512,64]{2,3,1,0:T(8,128)(2,1)} %param.4) | copy-start | bytes 1572868
  2.1 42.9 %all-to-all-start = ((bf16[8,1,2,64,512]{4,3,2,1,0:T(8,128)(2,1)}), bf16[8,1,2,64,512]{4,3,2,1,0:T(8,128)(2,1)}, u32[]{:S(2)}, u32[]{:S(2)}) async-start(bf16[8,1,2,64,512]{4,3,2,1,0:T(8,128)(2,1)} %broadcast_in_dim.39), calls=%async_computation | async-start | bytes 2097152 | tf_op jit(solution)/shard_map/all_to_all | solution.py:94
  8.6 29.4 %collective-permute-start.4 = (bf16[3,2,64,512]{3,2,1,0:T(8,128)(2,1)}, bf16[3,2,64,512]{3,2,1,0:T(8,128)(2,1)}, u32[]{:S(2)}, u32[]{:S(2)}) collective-permute-start(bf16[3,2,64,512]{3,2,1,0:T(8,128)(2,1)} %slice.104), channel_id=1, source_target_pairs={{0,256},{64,320},{128,384},{192,448},{256,0},{320,64},{384,128},{4... | collective-permute-start | bytes 1179656 | tf_op jit(solution)/shard_map/ppermute | solution.py:106
  10.5 20.2 %collective-permute-start.1 = (bf16[3,2,64,512]{3,2,1,0:T(8,128)(2,1)}, bf16[3,2,64,512]{3,2,1,0:T(8,128)(2,1)S(1)}, u32[]{:S(2)}, u32[]{:S(2)}) collective-permute-start(bf16[3,2,64,512]{3,2,1,0:T(8,128)(2,1)} %slice.104), channel_id=1, source_target_pairs={{0,192},{64,0},{128,64},{192,128},{256,448},{320,256},{384,320},{4... | collective-permute-start | bytes 1179656 | tf_op jit(solution)/shard_map/ppermute | solution.py:106
  15.7 19.6 %collective-permute-start = (bf16[3,2,64,512]{3,2,1,0:T(8,128)(2,1)}, bf16[3,2,64,512]{3,2,1,0:T(8,128)(2,1)S(1)}, u32[]{:S(2)}, u32[]{:S(2)}) collective-permute-start(bf16[3,2,64,512]{3,2,1,0:T(8,128)(2,1)} %slice.104), channel_id=1, source_target_pairs={{0,64},{64,128},{128,192},{192,0},{256,320},{320,384},{384,448},{4... | collective-permute-start | bytes 1179656 | tf_op jit(solution)/shard_map/ppermute | solution.py:106
  17.6 58.3 %collective-permute-start.7 = (bf16[3,2,64,512]{3,2,1,0:T(8,128)(2,1)}, bf16[3,2,64,512]{3,2,1,0:T(8,128)(2,1)}, u32[]{:S(2)}, u32[]{:S(2)}) collective-permute-start(bf16[3,2,64,512]{3,2,1,0:T(8,128)(2,1)} %slice.104), channel_id=1, source_target_pairs={{0,384},{64,448},{128,256},{192,320},{256,128},{320,192},{384,0},{... | collective-permute-start | bytes 1179656 | tf_op jit(solution)/shard_map/ppermute | solution.py:106
  31.4 37.2 %collective-permute-start.3 = (bf16[3,2,32,512]{3,2,1,0:T(8,128)(2,1)}, bf16[3,2,32,512]{3,2,1,0:T(8,128)(2,1)}, u32[]{:S(2)}, u32[]{:S(2)}) collective-permute-start(bf16[3,2,32,512]{3,2,1,0:T(8,128)(2,1)} %slice.106), channel_id=1, source_target_pairs={{0,192},{64,0},{128,64},{192,128},{256,448},{320,256},{384,320},{4... | collective-permute-start | bytes 589832 | tf_op jit(solution)/shard_map/ppermute | solution.py:106
  36.0 32.7 %collective-permute-start.2 = (bf16[3,2,32,512]{3,2,1,0:T(8,128)(2,1)}, bf16[3,2,32,512]{3,2,1,0:T(8,128)(2,1)}, u32[]{:S(2)}, u32[]{:S(2)}) collective-permute-start(bf16[3,2,32,512]{3,2,1,0:T(8,128)(2,1)} %slice.105), channel_id=1, source_target_pairs={{0,64},{64,128},{128,192},{192,0},{256,320},{320,384},{384,448},{4... | collective-permute-start | bytes 589832 | tf_op jit(solution)/shard_map/ppermute | solution.py:106
  38.0 36.2 %collective-permute-start.6 = (bf16[3,2,64,512]{3,2,1,0:T(8,128)(2,1)}, bf16[3,2,64,512]{3,2,1,0:T(8,128)(2,1)}, u32[]{:S(2)}, u32[]{:S(2)}) collective-permute-start(bf16[3,2,64,512]{3,2,1,0:T(8,128)(2,1)} %collective-permute-done.4), channel_id=1, source_target_pairs={{0,192},{64,0},{128,64},{192,128},{256,448},{320,256},{384,320},{4... | collective-permute-start | bytes 1179656 | tf_op jit(solution)/shard_map/ppermute | solution.py:106
  43.1 29.3 %collective-permute-start.5 = (bf16[3,2,64,512]{3,2,1,0:T(8,128)(2,1)}, bf16[3,2,64,512]{3,2,1,0:T(8,128)(2,1)}, u32[]{:S(2)}, u32[]{:S(2)}) collective-permute-start(bf16[3,2,64,512]{3,2,1,0:T(8,128)(2,1)} %collective-permute-done.4), channel_id=1, source_target_pairs={{0,64},{64,128},{128,192},{192,0},{256,320},{320,384},{384,448},{4... | collective-permute-start | bytes 1179656 | tf_op jit(solution)/shard_map/ppermute | solution.py:106
  48.5 52.2 %all-to-all-start.1 = ((bf16[64,1,2,8,256]{4,2,3,1,0:T(2,128)(2,1)}), bf16[64,1,2,8,256]{4,2,3,1,0:T(2,128)(2,1)S(1)}, u32[]{:S(2)}, u32[]{:S(2)}) async-start(bf16[64,1,2,8,256]{4,2,3,1,0:T(2,128)(2,1)} %bitcast.140), calls=%async_computation.1 | async-start | bytes 1048576 | tf_op jit(solution)/shard_map/all_to_all | solution.py:94
  68.6 9.1 %copy-start = (bf16[1,256,4,2,512]{4,1,3,0,2:T(8,128)(2,1)S(1)}, bf16[1,256,4,2,512]{4,1,3,0,2:T(8,128)(2,1)}, u32[]{:S(2)}) copy-start(bf16[1,256,4,2,512]{4,1,3,0,2:T(8,128)(2,1)} %maximum_bitcast_fusion) | copy-start | bytes 6291460
  82.8 23.4 %copy-start.4 = (f32[1024]{0:T(1024)S(1)}, f32[1024]{0:T(1024)}, u32[]{:S(2)}) copy-start(f32[1024]{0:T(1024)} %param.5) | copy-start | bytes 12292
  100.6 84.0 %all-to-all-start.2 = ((bf16[64,3,2,8,256]{4,3,2,1,0:T(8,128)(2,1)}), bf16[64,3,2,8,256]{4,3,2,1,0:T(8,128)(2,1)}, u32[]{:S(2)}, u32[]{:S(2)}) async-start(bf16[64,3,2,8,256]{4,3,2,1,0:T(8,128)(2,1)} %copy.60), calls=%async_computation.2 | async-start | bytes 3145728 | tf_op jit(solution)/shard_map/all_to_all | solution.py:94
  110.8 0.8 copy-start.1
  114.9 69.8 %copy-start.2 = (bf16[64,4,1,1024]{3,0,1,2:T(8,128)(2,1)S(1)}, bf16[64,4,1,1024]{3,0,1,2:T(8,128)(2,1)}, u32[]{:S(2)}) copy-start(bf16[64,4,1,1024]{3,0,1,2:T(8,128)(2,1)} %copy-done.1) | copy-start | bytes 1572868
  188.7 7.8 %collective-permute-start.8 = (f32[48,128]{1,0:T(8,128)S(1)}, f32[48,128]{1,0:T(8,128)S(1)}, u32[]{:S(2)}, u32[]{:S(2)}) collective-permute-start(f32[48,128]{1,0:T(8,128)S(1)} %bitcast.151), channel_id=1, source_target_pairs={{0,64},{64,128},{128,192},{192,256},{256,320},{320,384},{384,448},... | collective-permute-start | bytes 73736 | tf_op jit(solution)/shard_map/ppermute | solution.py:21

commit v2 on v1

--- a/solution.py
+++ b/solution.py
@@ -94,37 +94,44 @@
     return lax.all_to_all(block, axis, split_axis=0, concat_axis=0, tiled=True)
 
 
-def gathered_by_permutes(block):
+def across_tm(array, x_step, y_step):
     size = lax.axis_size("tm")
     ring = size // 2
+    route = [
+        (i, ((i // ring + y_step) % 2) * ring + (i % ring + x_step) % ring) for i in range(size)
+    ]
+    return lax.ppermute(array, "tm", route)
 
-    def moved(array, x_step, y_step):
-        route = [
-            (i, ((i // ring + y_step) % 2) * ring + (i % ring + x_step) % ring)
-            for i in range(size)
-        ]
-        return lax.ppermute(array, "tm", route)
 
-    half = block.shape[-2] // 2
-    left = moved(block, 1, 0)
-    right = moved(block, -1, 0)
-    across = moved(block, 0, 1)
-    far_a = moved(left[..., :half, :], 1, 0)
-    far_b = moved(right[..., half:, :], -1, 0)
-    across_left = moved(across, 1, 0)
-    across_right = moved(across, -1, 0)
-    across_far = moved(block, 2, 1)
-    far = jnp.concatenate([far_a, far_b], axis=-2)
+def own_row(block):
+    return (
+        across_tm(block, 1, 0),
+        across_tm(block, -1, 0),
+        across_tm(block, 0, 1),
+        across_tm(block, 2, 0),
+    )
+
+
+def whole_table(block, left, right, across, far):
+    across_left = across_tm(across, 1, 0)
+    across_right = across_tm(across, -1, 0)
+    across_far = across_tm(far, 0, 1)
+    size = lax.axis_size("tm")
+    ring = size // 2
     me = lax.axis_index("tm")
     y, x = me // ring, me % ring
-    table = jnp.zeros((size,) + block.shape, block.dtype)
+    table = jnp.broadcast_to(block[None], (size,) + block.shape)
     for piece, dx, dy in (
-        (block, 0, 0), (left, -1, 0), (right, 1, 0), (far, 2, 0),
-        (across, 0, 1), (across_left, -1, 1), (across_right, 1, 1), (across_far, 2, 1),
+        (left, -1, 0), (right, 1, 0), (across, 0, 1), (far, 2, 0),
+        (across_left, -1, 1), (across_right, 1, 1), (across_far, 2, 1),
     ):
         at = ((y + dy) % 2) * ring + (x + dx + ring) % ring
         table = lax.dynamic_update_slice(table, piece[None], (at,) + (0,) * block.ndim)
     return table
+
+
+def with_quadrature(samples):
+    return jnp.stack([samples, jnp.stack([samples[:, :, 1], -samples[:, :, 0]], axis=2)])
 
 
 def beam_form(samples, weights):
@@ -143,10 +150,12 @@
     size = lax.axis_size("tm")
     head = blocks[:HEAD]
     head = exchanged(jnp.broadcast_to(head[None], (size,) + head.shape), "tm")
-    both = jnp.stack([samples, jnp.stack([samples[:, :, 1], -samples[:, :, 0]], axis=2)])
-    head_spectra = exchanged(beam_form(both[:, :, :HEAD], head), "band")
-    rest = gathered_by_permutes(blocks[HEAD:])
-    rest_spectra = exchanged(beam_form(both[:, :, HEAD:], rest), "band")
+    row = own_row(blocks[HEAD:])
+    message = beam_form(with_quadrature(samples[:, :HEAD]), head)
+    head_spectra = exchanged(message, "band")
+    samples, row, block, _ = lax.optimization_barrier((samples, row, blocks[HEAD:], message))
+    rest = whole_table(block, *row)
+    rest_spectra = exchanged(beam_form(with_quadrature(samples[:, HEAD:]), rest), "band")
 
     table = synth_table(prototype)
     table = table.reshape((lax.axis_size("band"), -1) + table.shape[1:])

time: 199 us -> 180 us (0.905)
  local copies, waits for them, and re-layouts: 22.8 us -> 13.3 us
  waiting for transfers between devices: 91.9 us -> 86.9 us
  other arithmetic: 10.3 us -> 7.95 us
    all_to_all x3, waiting for transfers between devices: 87.5 us -> 77.2 us  [exchanged(): return lax.all_to_all(block, axis, split_axis=0, concat_axis=0, tiled=True)]
    ppermute x8 -> x7, waiting for transfers between devices: 1.14 us -> 6.68 us  [across_tm(): return lax.ppermute(array, 'tm', route)]
    dynamic_update_slice x7, local copies, waits for them, and re-layouts: 9.48 us -> 4.21 us  [whole_table(): lax.dynamic_update_slice(table, piece[None], (at,) + (0,) * block.ndim)]
    ppermute x8 -> x7, starting transfers between devices: 26.9 us -> 23.6 us  [across_tm(): return lax.ppermute(array, 'tm', route)]
    all_to_all x3, starting transfers between devices: 29.9 us -> 32.9 us  [exchanged(): return lax.all_to_all(block, axis, split_axis=0, concat_axis=0, tiled=True)]
    unnamed x11, local copies, waits for them, and re-layouts: 3.09 us -> 0.84 us
    another operation x2 -> x3, other arithmetic: 6.09 us -> 5.67 us
  transfers between devices with their start and end apart: 12 -> 11, of which waited for: 4 -> 5; matrix products, arithmetic and copies ran while one was open for 18% -> 12% of each run, Pallas kernels for 1% -> 1%
where the time goes in v2:
time: 180 us; the launch traced here: 179 us
  waiting for transfers between devices  86.9 us (48%)
  starting transfers between devices  58.7 us (33%)
  local copies, waits for them, and re-layouts  13.3 us (7%)
  matrix products  9.13 us (5%)
  other arithmetic  7.95 us (4%)
  Pallas kernels  2.56 us (1%)
    all_to_all x3, waiting for transfers between devices, exchanged(): return lax.all_to_all(block, axis, split_axis=0, concat_axis=0, tiled=True)  77.2 us
    all_to_all x3, starting transfers between devices, exchanged(): return lax.all_to_all(block, axis, split_axis=0, concat_axis=0, tiled=True)  32.9 us
    ppermute x7, starting transfers between devices, across_tm(): return lax.ppermute(array, 'tm', route)  23.6 us
    ppermute x7, waiting for transfers between devices, across_tm(): return lax.ppermute(array, 'tm', route)  6.68 us
    dot_general x2, matrix products, synthesize(): jnp.einsum('skcbf,skcm->bfm', spectra, part, preferred_element_type=jnp.f...  5.19 us
    another operation x1, other arithmetic  4.59 us
    dynamic_update_slice x7, local copies, waits for them, and re-layouts, whole_table(): lax.dynamic_update_slice(table, piece[None], (at,) + (0,) * block.ndim)  4.21 us
    dot_general x2, matrix products, beam_form(): jnp.einsum('pfkce,tkcbe->tbkpf', samples, weights, preferred_element_type...  3.94 us
  transfers between devices with their start and end apart: 11, of which 5 were waited for; matrix products, arithmetic and copies ran while one was open for 12% of the time, Pallas kernels for 1%

profile of v2, /device:TPU:24, one launch (start us, length us, event | category | flops | bytes accessed | tf_op | source)
XLA Modules:
  0.0 178.9 jit_solution(3749848035717695734)
XLA Ops:
  0.0 1.0 slice_bitcast_fusion.5
  1.0 1.1 broadcast_in_dim.39
  2.1 5.9 %all-to-all-start = ((bf16[8,1,2,64,512]{4,3,2,1,0:T(8,128)(2,1)}), bf16[8,1,2,64,512]{4,3,2,1,0:T(8,128)(2,1)}, u32[]{:S(2)}, u32[]{:S(2)}) async-start(bf16[8,1,2,64,512]{4,3,2,1,0:T(8,128)(2,1)} %broadcast_in_dim.39), calls=%async_computation | async-start | bytes 2097152 | tf_op jit(solution)/shard_map/all_to_all | solution.py:94
  8.0 3.4 %collective-permute-start = (bf16[3,2,64,512]{3,2,1,0:T(8,128)(2,1)S(1)}, bf16[3,2,64,512]{3,2,1,0:T(8,128)(2,1)}, u32[]{:S(2)}, u32[]{:S(2)}) collective-permute-start(bf16[3,2,64,512]{3,2,1,0:T(8,128)(2,1)S(1)} %slice.107), channel_id=1, source_target_pairs={{0,64},{64,128},{128,192},{192,0},{256,320},{320,384},{384,448},{4... | collective-permute-start | bytes 1179656 | tf_op jit(solution)/shard_map/ppermute | solution.py:103
  11.4 3.7 %collective-permute-start.1 = (bf16[3,2,64,512]{3,2,1,0:T(8,128)(2,1)S(1)}, bf16[3,2,64,512]{3,2,1,0:T(8,128)(2,1)}, u32[]{:S(2)}, u32[]{:S(2)}) collective-permute-start(bf16[3,2,64,512]{3,2,1,0:T(8,128)(2,1)S(1)} %slice.107), channel_id=1, source_target_pairs={{0,192},{64,0},{128,64},{192,128},{256,448},{320,256},{384,320},{4... | collective-permute-start | bytes 1179656 | tf_op jit(solution)/shard_map/ppermute | solution.py:103
  15.1 1.9 %collective-permute-start.2 = (bf16[3,2,64,512]{3,2,1,0:T(8,128)(2,1)S(1)}, bf16[3,2,64,512]{3,2,1,0:T(8,128)(2,1)}, u32[]{:S(2)}, u32[]{:S(2)}) collective-permute-start(bf16[3,2,64,512]{3,2,1,0:T(8,128)(2,1)S(1)} %slice.107), channel_id=1, source_target_pairs={{0,256},{64,320},{128,384},{192,448},{256,0},{320,64},{384,128},{4... | collective-permute-start | bytes 1179656 | tf_op jit(solution)/shard_map/ppermute | solution.py:103
  17.0 4.2 %collective-permute-start.3 = (bf16[3,2,64,512]{3,2,1,0:T(8,128)(2,1)S(1)}, bf16[3,2,64,512]{3,2,1,0:T(8,128)(2,1)}, u32[]{:S(2)}, u32[]{:S(2)}) collective-permute-start(bf16[3,2,64,512]{3,2,1,0:T(8,128)(2,1)S(1)} %slice.107), channel_id=1, source_target_pairs={{0,128},{64,192},{128,0},{192,64},{256,384},{320,448},{384,256},{4... | collective-permute-start | bytes 1179656 | tf_op jit(solution)/shard_map/ppermute | solution.py:103
  22.3 0.9 maximum_bitcast_fusion.9
  23.2 2.1 %fusion.10 = bf16[2,256,8,64]{1,3,2,0:T(8,128)(2,1)S(1)} fusion(bf16[1,256,1,2,512]{4,1,3,0,2:T(8,128)(2,1)S(1)} %get-tuple-element.36, bf16[1,256,1,2,512]{4,1,3,0,2:T(8,128)(2,1)} %get-tuple-element.37, bf16[8,1,2,64,512]{4,3,2,1,0:T(8,128)(2,1)} %all-to-all-done), kind=kOutput, calls=%fused_computation.21 | convolution fusion | flops 539230208 | bytes 2621440 | tf_op jit(solution)/shard_map/pfkce,tkcbe->tbkpf/dot_general | solution.py:138
  25.3 1.3 copy.97
  26.7 18.6 %all-to-all-start.1 = ((bf16[64,1,2,8,256]{4,2,3,1,0:T(2,128)(2,1)}), bf16[64,1,2,8,256]{4,2,3,1,0:T(2,128)(2,1)S(1)}, u32[]{:S(2)}, u32[]{:S(2)}) async-start(bf16[64,1,2,8,256]{4,2,3,1,0:T(2,128)(2,1)} %bitcast.138), calls=%async_computation.1 | async-start | bytes 1048576 | tf_op jit(solution)/shard_map/all_to_all | solution.py:94
  45.3 3.3 %collective-permute-start.4 = (bf16[3,2,64,512]{3,2,1,0:T(8,128)(2,1)}, bf16[3,2,64,512]{3,2,1,0:T(8,128)(2,1)S(1)}, u32[]{:S(2)}, u32[]{:S(2)}) collective-permute-start(bf16[3,2,64,512]{3,2,1,0:T(8,128)(2,1)} %collective-permute-done.2), channel_id=1, source_target_pairs={{0,64},{64,128},{128,192},{192,0},{256,320},{320,384},{384,448},{4... | collective-permute-start | bytes 1179656 | tf_op jit(solution)/shard_map/ppermute | solution.py:103
  48.7 3.7 %collective-permute-start.5 = (bf16[3,2,64,512]{3,2,1,0:T(8,128)(2,1)}, bf16[3,2,64,512]{3,2,1,0:T(8,128)(2,1)S(1)}, u32[]{:S(2)}, u32[]{:S(2)}) collective-permute-start(bf16[3,2,64,512]{3,2,1,0:T(8,128)(2,1)} %collective-permute-done.2), channel_id=1, source_target_pairs={{0,192},{64,0},{128,64},{192,128},{256,448},{320,256},{384,320},{4... | collective-permute-start | bytes 1179656 | tf_op jit(solution)/shard_map/ppermute | solution.py:103
  53.2 3.4 %collective-permute-start.6 = (bf16[3,2,64,512]{3,2,1,0:T(8,128)(2,1)}, bf16[3,2,64,512]{3,2,1,0:T(8,128)(2,1)S(1)}, u32[]{:S(2)}, u32[]{:S(2)}) collective-permute-start(bf16[3,2,64,512]{3,2,1,0:T(8,128)(2,1)} %collective-permute-done.3), channel_id=1, source_target_pairs={{0,256},{64,320},{128,384},{192,448},{256,0},{320,64},{384,128},{4... | collective-permute-start | bytes 1179656 | tf_op jit(solution)/shard_map/ppermute | solution.py:103
  57.0 1.0 bitcast_dynamic-update-slice_fusion.6
  58.0 1.0 bitcast_dynamic-update-slice_fusion.5
  59.0 1.0 bitcast_dynamic-update-slice_fusion.4
  60.2 1.0 bitcast_dynamic-update-slice_fusion.3
  61.7 6.5 %collective-permute-done.6 = bf16[3,2,64,512]{3,2,1,0:T(8,128)(2,1)S(1)} collective-permute-done((bf16[3,2,64,512]{3,2,1,0:T(8,128)(2,1)}, bf16[3,2,64,512]{3,2,1,0:T(8,128)(2,1)S(1)}, u32[]{:S(2)}, u32[]{:S(2)}) %collective-permute-start.6) | collective-permute-done | bytes 393248 | tf_op jit(solution)/shard_map/ppermute | solution.py:103
  68.2 1.8 %fusion.7 = bf16[8,64,3,2,256]{4,1,3,0,2:T(8,128)(2,1)S(1)} fusion(bf16[1,256,3,2,512]{4,1,3,0,2:T(8,128)(2,1)S(1)} %maximum_bitcast_fusion.4, bf16[1,256,3,2,512]{4,1,3,0,2:T(8,128)(2,1)S(1)} %slice_bitcast_fusion.4, bf16[8,3,2,64,512]{4,3,2,0,1:T(8,128)(2,1)S(1)} %bitcast_dynamic-update-slice_fusion), kind=kOutput, calls=%fused_computation.19 | convolution fusion | flops 1617690624 | bytes 7864320 | tf_op jit(solution)/shard_map/pfkce,tkcbe->tbkpf/dot_general | solution.py:138
  70.2 1.3 copy.66
  71.4 7.4 %all-to-all-done.1 = bf16[64,1,2,8,256]{4,2,3,1,0:T(2,128)(2,1)S(1)} async-done(((bf16[64,1,2,8,256]{4,2,3,1,0:T(2,128)(2,1)}), bf16[64,1,2,8,256]{4,2,3,1,0:T(2,128)(2,1)S(1)}, u32[]{:S(2)}, u32[]{:S(2)}) %all-to-all-start.1) | async-done | bytes 524320 | tf_op jit(solution)/shard_map/all_to_all | solution.py:94
  78.9 8.4 %all-to-all-start.2 = ((bf16[64,3,2,8,256]{4,3,2,1,0:T(8,128)(2,1)}), bf16[64,3,2,8,256]{4,3,2,1,0:T(8,128)(2,1)}, u32[]{:S(2)}, u32[]{:S(2)}) async-start(bf16[64,3,2,8,256]{4,3,2,1,0:T(8,128)(2,1)} %copy.66), calls=%async_computation.2 | async-start | bytes 3145728 | tf_op jit(solution)/shard_map/all_to_all | solution.py:94
  87.3 4.6 %multiply_convert_fusion.1 = (bf16[64,4,1,1024]{3,0,1,2:T(8,128)(2,1)S(1)}, bf16[64,4,1,1024]{3,0,1,2:T(8,128)(2,1)S(1)}) fusion(f32[1024]{0:T(1024)S(1)} %broadcast_multiply_fusion, s32[64,4]{0,1:T(4,128)S(1)} %add_add_fusion), kind=kLoop, calls=%fused_computation.30 | loop fusion | flops 4980736 | bytes 1053696 | tf_op jit(solution)/shard_map/convert
  92.9 1.3 convolution_bitcast_fusion.1
  94.2 0.9 slice_bitcast_fusion.3
  95.9 69.7 %all-to-all-done.2 = bf16[64,3,2,8,256]{4,3,2,1,0:T(8,128)(2,1)} async-done(((bf16[64,3,2,8,256]{4,3,2,1,0:T(8,128)(2,1)}), bf16[64,3,2,8,256]{4,3,2,1,0:T(8,128)(2,1)}, u32[]{:S(2)}, u32[]{:S(2)}) %all-to-all-start.2) | async-done | bytes 1572896 | tf_op jit(solution)/shard_map/all_to_all | solution.py:94
  165.7 3.9 %convolution_bitcast_fusion.frames_ref = f32[8,256,1024]{2,1,0:T(8,128)S(1)} fusion(bf16[64,3,2,8,256]{4,3,2,1,0:T(8,128)(2,1)} %all-to-all-done.2, bf16[64,4,1,1024]{3,0,1,2:T(8,128)(2,1)S(1)} %copy-done.2, bf16[64,4,1,1024]{3,0,1,2:T(8,128)(2,1)S(1)} %get-tuple-element.34), kind=kOutput, calls=%fused_computation | convolution fusion | flops 1611005952 | bytes 11010048 | tf_op jit(solution)/shard_map/skcbf,skcm->bfm/dot_general | solution.py:168
  169.7 2.2 %collective-permute-start.7 = (f32[48,128]{1,0:T(8,128)S(1)}, f32[48,128]{1,0:T(8,128)S(1)}, u32[]{:S(2)}, u32[]{:S(2)}) collective-permute-start(f32[48,128]{1,0:T(8,128)S(1)} %bitcast.145), channel_id=1, source_target_pairs={{0,64},{64,128},{128,192},{192,256},{256,320},{320,384},{384,448},... | collective-permute-start | bytes 73736 | tf_op jit(solution)/shard_map/ppermute | solution.py:21
  172.0 2.6 %overlap.1 = f32[4096,128]{1,0:T(8,128)} custom-call(f32[8,256,1024]{2,1,0:T(8,128)S(1)} %convolution_bitcast_fusion.frames_ref, f32[8,256,256]{2,1,0:T(8,128)S(1)} %slice.106.base_ref), custom_call_target="tpu_custom_call" | custom-call | flops 2097152 | bytes 12582912 | tf_op jit(solution)/shard_map/overlap/pallas_call | solution.py:78
  174.5 3.0 %collective-permute-done.7 = f32[48,128]{1,0:T(8,128)S(1)} collective-permute-done((f32[48,128]{1,0:T(8,128)S(1)}, f32[48,128]{1,0:T(8,128)S(1)}, u32[]{:S(2)}, u32[]{:S(2)}) %collective-permute-start.7) | collective-permute-done | bytes 24608 | tf_op jit(solution)/shard_map/ppermute | solution.py:21
  177.6 1.4 fusion.26
  (43 shorter events, 4.9 us)
Async XLA Ops:
  0.0 8.0 %copy-start.3 = (bf16[4,2,512,64]{2,3,1,0:T(8,128)(2,1)S(1)}, bf16[4,2,512,64]{2,3,1,0:T(8,128)(2,1)}, u32[]{:S(2)}) copy-start(bf16[4,2,512,64]{2,3,1,0:T(8,128)(2,1)} %param.4) | copy-start | bytes 1572868
  2.1 19.2 %copy-start = (bf16[256,4,2,512]{3,2,1,0:T(2,128)(2,1)S(1)}, bf16[256,4,2,512]{3,2,1,0:T(2,128)(2,1)}, u32[]{:S(2)}) copy-start(bf16[256,4,2,512]{3,2,1,0:T(2,128)(2,1)} %param.3) | copy-start | bytes 6291460
  2.1 21.1 %all-to-all-start = ((bf16[8,1,2,64,512]{4,3,2,1,0:T(8,128)(2,1)}), bf16[8,1,2,64,512]{4,3,2,1,0:T(8,128)(2,1)}, u32[]{:S(2)}, u32[]{:S(2)}) async-start(bf16[8,1,2,64,512]{4,3,2,1,0:T(8,128)(2,1)} %broadcast_in_dim.39), calls=%async_computation | async-start | bytes 2097152 | tf_op jit(solution)/shard_map/all_to_all | solution.py:94
  8.0 37.3 %collective-permute-start = (bf16[3,2,64,512]{3,2,1,0:T(8,128)(2,1)S(1)}, bf16[3,2,64,512]{3,2,1,0:T(8,128)(2,1)}, u32[]{:S(2)}, u32[]{:S(2)}) collective-permute-start(bf16[3,2,64,512]{3,2,1,0:T(8,128)(2,1)S(1)} %slice.107), channel_id=1, source_target_pairs={{0,64},{64,128},{128,192},{192,0},{256,320},{320,384},{384,448},{4... | collective-permute-start | bytes 1179656 | tf_op jit(solution)/shard_map/ppermute | solution.py:103
  11.4 33.9 %collective-permute-start.1 = (bf16[3,2,64,512]{3,2,1,0:T(8,128)(2,1)S(1)}, bf16[3,2,64,512]{3,2,1,0:T(8,128)(2,1)}, u32[]{:S(2)}, u32[]{:S(2)}) collective-permute-start(bf16[3,2,64,512]{3,2,1,0:T(8,128)(2,1)S(1)} %slice.107), channel_id=1, source_target_pairs={{0,192},{64,0},{128,64},{192,128},{256,448},{320,256},{384,320},{4... | collective-permute-start | bytes 1179656 | tf_op jit(solution)/shard_map/ppermute | solution.py:103
  15.1 30.3 %collective-permute-start.2 = (bf16[3,2,64,512]{3,2,1,0:T(8,128)(2,1)S(1)}, bf16[3,2,64,512]{3,2,1,0:T(8,128)(2,1)}, u32[]{:S(2)}, u32[]{:S(2)}) collective-permute-start(bf16[3,2,64,512]{3,2,1,0:T(8,128)(2,1)S(1)} %slice.107), channel_id=1, source_target_pairs={{0,256},{64,320},{128,384},{192,448},{256,0},{320,64},{384,128},{4... | collective-permute-start | bytes 1179656 | tf_op jit(solution)/shard_map/ppermute | solution.py:103
  17.0 28.3 %collective-permute-start.3 = (bf16[3,2,64,512]{3,2,1,0:T(8,128)(2,1)S(1)}, bf16[3,2,64,512]{3,2,1,0:T(8,128)(2,1)}, u32[]{:S(2)}, u32[]{:S(2)}) collective-permute-start(bf16[3,2,64,512]{3,2,1,0:T(8,128)(2,1)S(1)} %slice.107), channel_id=1, source_target_pairs={{0,128},{64,192},{128,0},{192,64},{256,384},{320,448},{384,256},{4... | collective-permute-start | bytes 1179656 | tf_op jit(solution)/shard_map/ppermute | solution.py:103
  21.2 1.0 slice-start
  26.7 52.2 %all-to-all-start.1 = ((bf16[64,1,2,8,256]{4,2,3,1,0:T(2,128)(2,1)}), bf16[64,1,2,8,256]{4,2,3,1,0:T(2,128)(2,1)S(1)}, u32[]{:S(2)}, u32[]{:S(2)}) async-start(bf16[64,1,2,8,256]{4,2,3,1,0:T(2,128)(2,1)} %bitcast.138), calls=%async_computation.1 | async-start | bytes 1048576 | tf_op jit(solution)/shard_map/all_to_all | solution.py:94
  45.3 16.1 %collective-permute-start.4 = (bf16[3,2,64,512]{3,2,1,0:T(8,128)(2,1)}, bf16[3,2,64,512]{3,2,1,0:T(8,128)(2,1)S(1)}, u32[]{:S(2)}, u32[]{:S(2)}) collective-permute-start(bf16[3,2,64,512]{3,2,1,0:T(8,128)(2,1)} %collective-permute-done.2), channel_id=1, source_target_pairs={{0,64},{64,128},{128,192},{192,0},{256,320},{320,384},{384,448},{4... | collective-permute-start | bytes 1179656 | tf_op jit(solution)/shard_map/ppermute | solution.py:103
  48.7 13.0 %collective-permute-start.5 = (bf16[3,2,64,512]{3,2,1,0:T(8,128)(2,1)}, bf16[3,2,64,512]{3,2,1,0:T(8,128)(2,1)S(1)}, u32[]{:S(2)}, u32[]{:S(2)}) collective-permute-start(bf16[3,2,64,512]{3,2,1,0:T(8,128)(2,1)} %collective-permute-done.2), channel_id=1, source_target_pairs={{0,192},{64,0},{128,64},{192,128},{256,448},{320,256},{384,320},{4... | collective-permute-start | bytes 1179656 | tf_op jit(solution)/shard_map/ppermute | solution.py:103
  53.2 15.0 %collective-permute-start.6 = (bf16[3,2,64,512]{3,2,1,0:T(8,128)(2,1)}, bf16[3,2,64,512]{3,2,1,0:T(8,128)(2,1)S(1)}, u32[]{:S(2)}, u32[]{:S(2)}) collective-permute-start(bf16[3,2,64,512]{3,2,1,0:T(8,128)(2,1)} %collective-permute-done.3), channel_id=1, source_target_pairs={{0,256},{64,320},{128,384},{192,448},{256,0},{320,64},{384,128},{4... | collective-permute-start | bytes 1179656 | tf_op jit(solution)/shard_map/ppermute | solution.py:103
  71.4 15.8 %copy-start.4 = (f32[1024]{0:T(1024)S(1)}, f32[1024]{0:T(1024)}, u32[]{:S(2)}) copy-start(f32[1024]{0:T(1024)} %param.5) | copy-start | bytes 12292
  78.9 86.8 %all-to-all-start.2 = ((bf16[64,3,2,8,256]{4,3,2,1,0:T(8,128)(2,1)}), bf16[64,3,2,8,256]{4,3,2,1,0:T(8,128)(2,1)}, u32[]{:S(2)}, u32[]{:S(2)}) async-start(bf16[64,3,2,8,256]{4,3,2,1,0:T(8,128)(2,1)} %copy.66), calls=%async_computation.2 | async-start | bytes 3145728 | tf_op jit(solution)/shard_map/all_to_all | solution.py:94
  91.9 0.8 copy-start.1
  95.9 69.8 %copy-start.2 = (bf16[64,4,1,1024]{3,0,1,2:T(8,128)(2,1)S(1)}, bf16[64,4,1,1024]{3,0,1,2:T(8,128)(2,1)}, u32[]{:S(2)}) copy-start(bf16[64,4,1,1024]{3,0,1,2:T(8,128)(2,1)} %copy-done.1) | copy-start | bytes 1572868
  169.7 7.8 %collective-permute-start.7 = (f32[48,128]{1,0:T(8,128)S(1)}, f32[48,128]{1,0:T(8,128)S(1)}, u32[]{:S(2)}, u32[]{:S(2)}) collective-permute-start(f32[48,128]{1,0:T(8,128)S(1)} %bitcast.145), channel_id=1, source_target_pairs={{0,64},{64,128},{128,192},{192,256},{256,320},{320,384},{384,448},... | collective-permute-start | bytes 73736 | tf_op jit(solution)/shard_map/ppermute | solution.py:21

commit v3 on v2

--- a/solution.py
+++ b/solution.py
@@ -12,6 +12,7 @@
 K = 256
 FIRST_BIN = 32
 LANES = 128
+PLANE = 4
 HEAD = 1
 
 
@@ -94,6 +95,35 @@
     return lax.all_to_all(block, axis, split_axis=0, concat_axis=0, tiled=True)
 
 
+def along_z(block):
+    size = lax.axis_size("band")
+    groups = [list(range(place, size, PLANE)) for place in range(PLANE)]
+    return lax.all_to_all(
+        block, "band", split_axis=0, concat_axis=0, tiled=True, axis_index_groups=groups
+    )
+
+
+def in_planes(array):
+    return array.reshape((-1, PLANE) + array.shape[1:])
+
+
+def by_distance(array):
+    place = lax.axis_index("band") % PLANE
+    return [
+        lax.dynamic_index_in_dim(array, place ^ step, axis=1, keepdims=False)
+        for step in range(PLANE)
+    ]
+
+
+def within_plane(array):
+    size = lax.axis_size("band")
+    pieces = by_distance(array)
+    for step in range(1, PLANE):
+        route = [(i, i ^ step) for i in range(size)]
+        pieces[step] = lax.ppermute(pieces[step], "band", route)
+    return jnp.stack(pieces, axis=1)
+
+
 def across_tm(array, x_step, y_step):
     size = lax.axis_size("tm")
     ring = size // 2
@@ -134,14 +164,27 @@
     return jnp.stack([samples, jnp.stack([samples[:, :, 1], -samples[:, :, 0]], axis=2)])
 
 
-def beam_form(samples, weights):
+def beam_form_of_pairs(samples, weights):
     products = jnp.einsum(
-        "pfkce,tkcbe->tbkpf", samples, weights, preferred_element_type=jnp.float32
-    )
+        "fkce,tkdbe->tbkdcf", samples, weights, preferred_element_type=jnp.float32
+    )
+    real_part = products[:, :, :, 0, 0] + products[:, :, :, 1, 1]
+    imag_part = products[:, :, :, 0, 1] - products[:, :, :, 1, 0]
+    return to_messages(jnp.stack([real_part, imag_part], axis=3))
+
+
+def to_messages(products):
     spectra = products.astype(jnp.bfloat16)
     size = lax.axis_size("band")
     spectra = spectra.reshape((size, -1) + spectra.shape[2:])
     return jnp.transpose(spectra, (0, 2, 3, 1, 4))
+
+
+def beam_form(samples, weights):
+    products = jnp.einsum(
+        "pfkce,tkcbe->tbkpf", samples, weights, preferred_element_type=jnp.float32
+    )
+    return to_messages(products)
 
 
 def shards(samples, weights, prototype):
@@ -151,11 +194,13 @@
     head = blocks[:HEAD]
     head = exchanged(jnp.broadcast_to(head[None], (size,) + head.shape), "tm")
     row = own_row(blocks[HEAD:])
-    message = beam_form(with_quadrature(samples[:, :HEAD]), head)
-    head_spectra = exchanged(message, "band")
+    message = beam_form_of_pairs(samples[:, :HEAD], head)
+    head_spectra = along_z(in_planes(message))
     samples, row, block, _ = lax.optimization_barrier((samples, row, blocks[HEAD:], message))
     rest = whole_table(block, *row)
-    rest_spectra = exchanged(beam_form(with_quadrature(samples[:, HEAD:]), rest), "band")
+    rest_message = beam_form(with_quadrature(samples[:, HEAD:]), rest)
+    rest_spectra = exchanged(rest_message, "band")
+    head_spectra = within_plane(head_spectra).reshape(message.shape)
 
     table = synth_table(prototype)
     table = table.reshape((lax.axis_size("band"), -1) + table.shape[1:])
@@ -178,7 +223,9 @@
             )
         return jnp.stack(rows)
 
-    base = intersection_add(synthesize(head_spectra, table[:, :HEAD]), hop_size)
+    head_table = jnp.stack(by_distance(in_planes(table[:, :HEAD])), axis=1)
+    head_table = head_table.reshape(table[:, :HEAD].shape)
+    base = intersection_add(synthesize(head_spectra, head_table), hop_size)
     base, spill = base[:, :frame_total], base[:, frame_total:]
     base, spill, rest_spectra = lax.optimization_barrier((base, spill, rest_spectra))
     rest_frames = synthesize(rest_spectra, table[:, HEAD:])

time: 180 us -> 187 us (1.039)
  starting transfers between devices: 58.7 us -> 67 us
  waiting for transfers between devices: 86.9 us -> 80.1 us
  local copies, waits for them, and re-layouts: 13.3 us -> 18.1 us
  other arithmetic: 7.95 us -> 10.4 us
    all_to_all x3 -> x2, waiting for transfers between devices: 77.2 us -> 55.2 us  [exchanged(): return lax.all_to_all(block, axis, split_axis=0, concat_axis=0, tiled=True)]
    all_to_all x3 -> x2, starting transfers between devices: 32.9 us -> 15 us  [exchanged(): return lax.all_to_all(block, axis, split_axis=0, concat_axis=0, tiled=True)]
    all_to_all x0 -> x1, waiting for transfers between devices: none -> 16 us  [along_z(): lax.all_to_all(block, 'band', split_axis=0, concat_axis=0, tiled=True, ax...]
    all_to_all x0 -> x1, starting transfers between devices: none -> 15.4 us  [along_z(): lax.all_to_all(block, 'band', split_axis=0, concat_axis=0, tiled=True, ax...]
    ppermute x0 -> x3, starting transfers between devices: none -> 9.27 us  [within_plane(): pieces[step] = lax.ppermute(pieces[step], 'band', route)]
    dynamic_update_slice x7, local copies, waits for them, and re-layouts: 4.21 us -> 7.35 us  [whole_table(): lax.dynamic_update_slice(table, piece[None], (at,) + (0,) * block.ndim)]
    ppermute x0 -> x3, waiting for transfers between devices: none -> 2.8 us  [within_plane(): pieces[step] = lax.ppermute(pieces[step], 'band', route)]
    ppermute x7, waiting for transfers between devices: 6.68 us -> 3.94 us  [across_tm(): return lax.ppermute(array, 'tm', route)]
  transfers between devices with their start and end apart: 11 -> 14, of which waited for: 5 -> 6; matrix products, arithmetic and copies ran while one was open for 12% -> 15% of each run, Pallas kernels for 1% -> 1%
where the time goes in v3:
time: 187 us; the launch traced here: 186 us
  waiting for transfers between devices  80.1 us (43%)
  starting transfers between devices  67 us (36%)
  local copies, waits for them, and re-layouts  18.1 us (10%)
  other arithmetic  10.4 us (6%)
  matrix products  7.73 us (4%)
  Pallas kernels  2.56 us (1%)
    all_to_all x2, waiting for transfers between devices, exchanged(): return lax.all_to_all(block, axis, split_axis=0, concat_axis=0, tiled=True)  55.2 us
    ppermute x7, starting transfers between devices, across_tm(): return lax.ppermute(array, 'tm', route)  24.2 us
    all_to_all x1, waiting for transfers between devices, along_z(): lax.all_to_all(block, 'band', split_axis=0, concat_axis=0, tiled=True, ax...  16 us
    all_to_all x1, starting transfers between devices, along_z(): lax.all_to_all(block, 'band', split_axis=0, concat_axis=0, tiled=True, ax...  15.4 us
    all_to_all x2, starting transfers between devices, exchanged(): return lax.all_to_all(block, axis, split_axis=0, concat_axis=0, tiled=True)  15 us
    ppermute x3, starting transfers between devices, within_plane(): pieces[step] = lax.ppermute(pieces[step], 'band', route)  9.27 us
    dynamic_update_slice x7, local copies, waits for them, and re-layouts, whole_table(): lax.dynamic_update_slice(table, piece[None], (at,) + (0,) * block.ndim)  7.35 us
    dot_general x2, matrix products, synthesize(): jnp.einsum('skcbf,skcm->bfm', spectra, part, preferred_element_type=jnp.f...  5.16 us
  transfers between devices with their start and end apart: 14, of which 6 were waited for; matrix products, arithmetic and copies ran while one was open for 15% of the time, Pallas kernels for 1%

profile of v3, /device:TPU:24, one launch (start us, length us, event | category | flops | bytes accessed | tf_op | source)
XLA Modules:
  0.0 186.5 jit_solution(11644690604755028018)
XLA Ops:
  1.0 3.4 %collective-permute-start.3 = (bf16[3,2,64,512]{3,2,1,0:T(8,128)(2,1)S(1)}, bf16[3,2,64,512]{3,2,1,0:T(8,128)(2,1)}, u32[]{:S(2)}, u32[]{:S(2)}) collective-permute-start(bf16[3,2,64,512]{3,2,1,0:T(8,128)(2,1)S(1)} %slice.117), channel_id=1, source_target_pairs={{0,64},{64,128},{128,192},{192,0},{256,320},{320,384},{384,448},{4... | collective-permute-start | bytes 1179656 | tf_op jit(solution)/shard_map/ppermute | solution.py:133
  4.4 3.7 %collective-permute-start.4 = (bf16[3,2,64,512]{3,2,1,0:T(8,128)(2,1)S(1)}, bf16[3,2,64,512]{3,2,1,0:T(8,128)(2,1)}, u32[]{:S(2)}, u32[]{:S(2)}) collective-permute-start(bf16[3,2,64,512]{3,2,1,0:T(8,128)(2,1)S(1)} %slice.117), channel_id=1, source_target_pairs={{0,192},{64,0},{128,64},{192,128},{256,448},{320,256},{384,320},{4... | collective-permute-start | bytes 1179656 | tf_op jit(solution)/shard_map/ppermute | solution.py:133
  8.1 2.7 %collective-permute-start.5 = (bf16[3,2,64,512]{3,2,1,0:T(8,128)(2,1)S(1)}, bf16[3,2,64,512]{3,2,1,0:T(8,128)(2,1)}, u32[]{:S(2)}, u32[]{:S(2)}) collective-permute-start(bf16[3,2,64,512]{3,2,1,0:T(8,128)(2,1)S(1)} %slice.117), channel_id=1, source_target_pairs={{0,256},{64,320},{128,384},{192,448},{256,0},{320,64},{384,128},{4... | collective-permute-start | bytes 1179656 | tf_op jit(solution)/shard_map/ppermute | solution.py:133
  10.8 3.7 %collective-permute-start.6 = (bf16[3,2,64,512]{3,2,1,0:T(8,128)(2,1)S(1)}, bf16[3,2,64,512]{3,2,1,0:T(8,128)(2,1)}, u32[]{:S(2)}, u32[]{:S(2)}) collective-permute-start(bf16[3,2,64,512]{3,2,1,0:T(8,128)(2,1)S(1)} %slice.117), channel_id=1, source_target_pairs={{0,128},{64,192},{128,0},{192,64},{256,384},{320,448},{384,256},{4... | collective-permute-start | bytes 1179656 | tf_op jit(solution)/shard_map/ppermute | solution.py:133
  15.4 1.1 broadcast_in_dim.39
  16.5 4.8 %all-to-all-start = ((bf16[8,1,2,64,512]{4,3,2,1,0:T(8,128)(2,1)}), bf16[8,1,2,64,512]{4,3,2,1,0:T(8,128)(2,1)S(1)}, u32[]{:S(2)}, u32[]{:S(2)}) async-start(bf16[8,1,2,64,512]{4,3,2,1,0:T(8,128)(2,1)} %broadcast_in_dim.39), calls=%async_computation | async-start | bytes 2097152 | tf_op jit(solution)/shard_map/all_to_all | solution.py:95
  21.3 2.0 %collective-permute-done.4 = bf16[3,2,64,512]{3,2,1,0:T(8,128)(2,1)} collective-permute-done((bf16[3,2,64,512]{3,2,1,0:T(8,128)(2,1)S(1)}, bf16[3,2,64,512]{3,2,1,0:T(8,128)(2,1)}, u32[]{:S(2)}, u32[]{:S(2)}) %collective-permute-start.4) | collective-permute-done | bytes 393248 | tf_op jit(solution)/shard_map/ppermute | solution.py:133
  23.3 1.9 %collective-permute-done.6 = bf16[3,2,64,512]{3,2,1,0:T(8,128)(2,1)} collective-permute-done((bf16[3,2,64,512]{3,2,1,0:T(8,128)(2,1)S(1)}, bf16[3,2,64,512]{3,2,1,0:T(8,128)(2,1)}, u32[]{:S(2)}, u32[]{:S(2)}) %collective-permute-start.6) | collective-permute-done | bytes 393248 | tf_op jit(solution)/shard_map/ppermute | solution.py:133
  25.2 5.7 %collective-permute-start.7 = (bf16[3,2,64,512]{3,2,1,0:T(8,128)(2,1)}, bf16[3,2,64,512]{3,2,1,0:T(8,128)(2,1)}, u32[]{:S(2)}, u32[]{:S(2)}) collective-permute-start(bf16[3,2,64,512]{3,2,1,0:T(8,128)(2,1)} %collective-permute-done.5), channel_id=1, source_target_pairs={{0,64},{64,128},{128,192},{192,0},{256,320},{320,384},{384,448},{4... | collective-permute-start | bytes 1179656 | tf_op jit(solution)/shard_map/ppermute | solution.py:133
  30.9 2.5 %collective-permute-start.8 = (bf16[3,2,64,512]{3,2,1,0:T(8,128)(2,1)}, bf16[3,2,64,512]{3,2,1,0:T(8,128)(2,1)}, u32[]{:S(2)}, u32[]{:S(2)}) collective-permute-start(bf16[3,2,64,512]{3,2,1,0:T(8,128)(2,1)} %collective-permute-done.5), channel_id=1, source_target_pairs={{0,192},{64,0},{128,64},{192,128},{256,448},{320,256},{384,320},{4... | collective-permute-start | bytes 1179656 | tf_op jit(solution)/shard_map/ppermute | solution.py:133
  34.1 2.7 %collective-permute-start.9 = (bf16[3,2,64,512]{3,2,1,0:T(8,128)(2,1)}, bf16[3,2,64,512]{3,2,1,0:T(8,128)(2,1)}, u32[]{:S(2)}, u32[]{:S(2)}) collective-permute-start(bf16[3,2,64,512]{3,2,1,0:T(8,128)(2,1)} %collective-permute-done.6), channel_id=1, source_target_pairs={{0,256},{64,320},{128,384},{192,448},{256,0},{320,64},{384,128},{4... | collective-permute-start | bytes 1179656 | tf_op jit(solution)/shard_map/ppermute | solution.py:133
  38.3 1.5 copy-done.1
  39.8 1.9 %slice_bitcast_fusion.4 = (bf16[1,256,3,2,512]{4,1,3,0,2:T(8,128)(2,1)}, bf16[1,256,3,2,512]{4,1,3,0,2:T(8,128)(2,1)}) fusion(bf16[256,4,2,512]{3,0,2,1:T(8,128)(2,1)S(1)} %copy.87, bf16[256,3,1,512]{3,0,2,1:T(8,128)(2,1)S(1)} %get-tuple-element.28, bf16[256,3,1,512]{3,0,2,1:T(8,128)(2,1)S(1)} %get-tuple-element.27), kind=kLoop, calls=%fused_computation.14 | loop fusion | flops 786432 | bytes 6291456 | tf_op jit(solution)/shard_map/stack | solution.py:164
  43.5 15.4 %all-to-all-start.1 = ((bf16[16,4,1,2,8,256]{5,4,3,1,2,0:T(8,128)(2,1)}), bf16[16,4,1,2,8,256]{5,4,3,1,2,0:T(8,128)(2,1)}, u32[]{:S(2)}, u32[]{:S(2)}) async-start(bf16[16,4,1,2,8,256]{5,4,3,1,2,0:T(8,128)(2,1)} %bitcast.162), calls=%async_computation.1 | async-start | bytes 1048576 | tf_op jit(solution)/shard_map/all_to_all | solution.py:101
  59.9 1.2 bitcast_dynamic-update-slice_fusion.4
  65.3 1.8 fusion.7
  67.3 1.3 copy.91
  68.5 16.0 %all-to-all-done.1 = bf16[16,4,1,2,8,256]{5,4,3,1,2,0:T(8,128)(2,1)} async-done(((bf16[16,4,1,2,8,256]{5,4,3,1,2,0:T(8,128)(2,1)}), bf16[16,4,1,2,8,256]{5,4,3,1,2,0:T(8,128)(2,1)}, u32[]{:S(2)}, u32[]{:S(2)}) %all-to-all-start.1) | async-done | bytes 524320 | tf_op jit(solution)/shard_map/all_to_all | solution.py:101
  84.5 10.3 %all-to-all-start.2 = ((bf16[64,3,2,8,256]{4,3,2,1,0:T(8,128)(2,1)}), bf16[64,3,2,8,256]{4,3,2,1,0:T(8,128)(2,1)}, u32[]{:S(2)}, u32[]{:S(2)}) async-start(bf16[64,3,2,8,256]{4,3,2,1,0:T(8,128)(2,1)} %copy.91), calls=%async_computation.2 | async-start | bytes 3145728 | tf_op jit(solution)/shard_map/all_to_all | solution.py:95
  94.8 4.6 %multiply_convert_fusion.1 = (bf16[64,4,1,1024]{3,0,1,2:T(8,128)(2,1)S(1)}, bf16[64,4,1,1024]{3,0,1,2:T(8,128)(2,1)S(1)}) fusion(f32[1024]{0:T(1024)S(1)} %broadcast_multiply_fusion, s32[64,4]{0,1:T(4,128)S(1)} %add_add_fusion), kind=kLoop, calls=%fused_computation.26 | loop fusion | flops 4980736 | bytes 1053696 | tf_op jit(solution)/shard_map/convert
  99.6 1.1 dynamic-slice_bitcast_fusion.3
  100.8 2.0 %collective-permute-start.2 = (bf16[16,1,2,8,256]{4,3,2,0,1:T(8,128)(2,1)S(1)}, bf16[16,1,2,8,256]{4,3,2,0,1:T(8,128)(2,1)S(1)}, u32[]{:S(2)}, u32[]{:S(2)}) collective-permute-start(bf16[16,1,2,8,256]{4,3,2,0,1:T(8,128)(2,1)S(1)} %get-tuple-element.34), channel_id=1, source_target_pairs={{0,3},{1,2},{2,1},{3,0},{4,7},{5,6},{6,5},{7,4},{8,11},{9,10},{10,... | collective-permute-start | bytes 393224 | tf_op jit(solution)/shard_map/ppermute | solution.py:123
  102.8 5.0 %collective-permute-start.1 = (bf16[16,1,2,8,256]{4,3,2,0,1:T(8,128)(2,1)S(1)}, bf16[16,1,2,8,256]{4,3,2,0,1:T(8,128)(2,1)S(1)}, u32[]{:S(2)}, u32[]{:S(2)}) collective-permute-start(bf16[16,1,2,8,256]{4,3,2,0,1:T(8,128)(2,1)S(1)} %get-tuple-element.32), channel_id=1, source_target_pairs={{0,2},{1,3},{2,0},{3,1},{4,6},{5,7},{6,4},{7,5},{8,10},{9,11},{10,... | collective-permute-start | bytes 393224 | tf_op jit(solution)/shard_map/ppermute | solution.py:123
  107.8 2.2 %collective-permute-start = (bf16[16,1,2,8,256]{4,3,2,0,1:T(8,128)(2,1)S(1)}, bf16[16,1,2,8,256]{4,3,2,0,1:T(8,128)(2,1)S(1)}, u32[]{:S(2)}, u32[]{:S(2)}) collective-permute-start(bf16[16,1,2,8,256]{4,3,2,0,1:T(8,128)(2,1)S(1)} %get-tuple-element.33), channel_id=1, source_target_pairs={{0,1},{1,0},{2,3},{3,2},{4,5},{5,4},{6,7},{7,6},{8,9},{9,8},{10,11... | collective-permute-start | bytes 393224 | tf_op jit(solution)/shard_map/ppermute | solution.py:123
  111.6 2.8 %collective-permute-done.1 = bf16[16,1,2,8,256]{4,3,2,0,1:T(8,128)(2,1)S(1)} collective-permute-done((bf16[16,1,2,8,256]{4,3,2,0,1:T(8,128)(2,1)S(1)}, bf16[16,1,2,8,256]{4,3,2,0,1:T(8,128)(2,1)S(1)}, u32[]{:S(2)}, u32[]{:S(2)}) %collective-permute-start.1) | collective-permute-done | bytes 131104 | tf_op jit(solution)/shard_map/ppermute | solution.py:123
  115.0 1.3 convolution_bitcast_fusion.1
  118.0 55.2 %all-to-all-done.2 = bf16[64,3,2,8,256]{4,3,2,1,0:T(8,128)(2,1)} async-done(((bf16[64,3,2,8,256]{4,3,2,1,0:T(8,128)(2,1)}), bf16[64,3,2,8,256]{4,3,2,1,0:T(8,128)(2,1)}, u32[]{:S(2)}, u32[]{:S(2)}) %all-to-all-start.2) | async-done | bytes 1572896 | tf_op jit(solution)/shard_map/all_to_all | solution.py:95
  173.2 3.9 %convolution_bitcast_fusion.frames_ref = f32[8,256,1024]{2,1,0:T(8,128)S(1)} fusion(bf16[64,3,2,8,256]{4,3,2,1,0:T(8,128)(2,1)} %all-to-all-done.2, bf16[64,4,1,1024]{3,0,1,2:T(8,128)(2,1)S(1)} %get-tuple-element.43, bf16[64,4,1,1024]{3,0,1,2:T(8,128)(2,1)S(1)} %get-tuple-element.42), kind=kOutput, calls=%fused_computation | convolution fusion | flops 1611005952 | bytes 11010048 | tf_op jit(solution)/shard_map/skcbf,skcm->bfm/dot_general | solution.py:213
  177.3 3.1 %collective-permute-start.10 = (f32[48,128]{1,0:T(8,128)S(1)}, f32[48,128]{1,0:T(8,128)S(1)}, u32[]{:S(2)}, u32[]{:S(2)}) collective-permute-start(f32[48,128]{1,0:T(8,128)S(1)} %bitcast.173), channel_id=1, source_target_pairs={{0,64},{64,128},{128,192},{192,256},{256,320},{320,384},{384,448},... | collective-permute-start | bytes 73736 | tf_op jit(solution)/shard_map/ppermute | solution.py:22
  180.4 2.6 %overlap.1 = f32[4096,128]{1,0:T(8,128)} custom-call(f32[8,256,1024]{2,1,0:T(8,128)S(1)} %convolution_bitcast_fusion.frames_ref, f32[8,256,256]{2,1,0:T(8,128)S(1)} %slice.116.base_ref), custom_call_target="tpu_custom_call" | custom-call | flops 2097152 | bytes 12582912 | tf_op jit(solution)/shard_map/overlap/pallas_call | solution.py:79
  182.9 2.2 %collective-permute-done.10 = f32[48,128]{1,0:T(8,128)S(1)} collective-permute-done((f32[48,128]{1,0:T(8,128)S(1)}, f32[48,128]{1,0:T(8,128)S(1)}, u32[]{:S(2)}, u32[]{:S(2)}) %collective-permute-start.10) | collective-permute-done | bytes 24608 | tf_op jit(solution)/shard_map/ppermute | solution.py:22
  185.1 1.4 fusion.23
  (55 shorter events, 15.2 us)
Async XLA Ops:
  1.0 20.3 %collective-permute-start.3 = (bf16[3,2,64,512]{3,2,1,0:T(8,128)(2,1)S(1)}, bf16[3,2,64,512]{3,2,1,0:T(8,128)(2,1)}, u32[]{:S(2)}, u32[]{:S(2)}) collective-permute-start(bf16[3,2,64,512]{3,2,1,0:T(8,128)(2,1)S(1)} %slice.117), channel_id=1, source_target_pairs={{0,64},{64,128},{128,192},{192,0},{256,320},{320,384},{384,448},{4... | collective-permute-start | bytes 1179656 | tf_op jit(solution)/shard_map/ppermute | solution.py:133
  4.4 18.8 %collective-permute-start.4 = (bf16[3,2,64,512]{3,2,1,0:T(8,128)(2,1)S(1)}, bf16[3,2,64,512]{3,2,1,0:T(8,128)(2,1)}, u32[]{:S(2)}, u32[]{:S(2)}) collective-permute-start(bf16[3,2,64,512]{3,2,1,0:T(8,128)(2,1)S(1)} %slice.117), channel_id=1, source_target_pairs={{0,192},{64,0},{128,64},{192,128},{256,448},{320,256},{384,320},{4... | collective-permute-start | bytes 1179656 | tf_op jit(solution)/shard_map/ppermute | solution.py:133
  8.1 15.2 %collective-permute-start.5 = (bf16[3,2,64,512]{3,2,1,0:T(8,128)(2,1)S(1)}, bf16[3,2,64,512]{3,2,1,0:T(8,128)(2,1)}, u32[]{:S(2)}, u32[]{:S(2)}) collective-permute-start(bf16[3,2,64,512]{3,2,1,0:T(8,128)(2,1)S(1)} %slice.117), channel_id=1, source_target_pairs={{0,256},{64,320},{128,384},{192,448},{256,0},{320,64},{384,128},{4... | collective-permute-start | bytes 1179656 | tf_op jit(solution)/shard_map/ppermute | solution.py:133
  10.8 14.5 %collective-permute-start.6 = (bf16[3,2,64,512]{3,2,1,0:T(8,128)(2,1)S(1)}, bf16[3,2,64,512]{3,2,1,0:T(8,128)(2,1)}, u32[]{:S(2)}, u32[]{:S(2)}) collective-permute-start(bf16[3,2,64,512]{3,2,1,0:T(8,128)(2,1)S(1)} %slice.117), channel_id=1, source_target_pairs={{0,128},{64,192},{128,0},{192,64},{256,384},{320,448},{384,256},{4... | collective-permute-start | bytes 1179656 | tf_op jit(solution)/shard_map/ppermute | solution.py:133
  15.4 18.0 %copy-start = (bf16[256,4,2,512]{3,2,1,0:T(2,128)(2,1)S(1)}, bf16[256,4,2,512]{3,2,1,0:T(2,128)(2,1)}, u32[]{:S(2)}) copy-start(bf16[256,4,2,512]{3,2,1,0:T(2,128)(2,1)} %param.3) | copy-start | bytes 6291460
  16.5 25.2 %all-to-all-start = ((bf16[8,1,2,64,512]{4,3,2,1,0:T(8,128)(2,1)}), bf16[8,1,2,64,512]{4,3,2,1,0:T(8,128)(2,1)S(1)}, u32[]{:S(2)}, u32[]{:S(2)}) async-start(bf16[8,1,2,64,512]{4,3,2,1,0:T(8,128)(2,1)} %broadcast_in_dim.39), calls=%async_computation | async-start | bytes 2097152 | tf_op jit(solution)/shard_map/all_to_all | solution.py:95
  25.2 36.9 %collective-permute-start.7 = (bf16[3,2,64,512]{3,2,1,0:T(8,128)(2,1)}, bf16[3,2,64,512]{3,2,1,0:T(8,128)(2,1)}, u32[]{:S(2)}, u32[]{:S(2)}) collective-permute-start(bf16[3,2,64,512]{3,2,1,0:T(8,128)(2,1)} %collective-permute-done.5), channel_id=1, source_target_pairs={{0,64},{64,128},{128,192},{192,0},{256,320},{320,384},{384,448},{4... | collective-permute-start | bytes 1179656 | tf_op jit(solution)/shard_map/ppermute | solution.py:133
  30.9 32.3 %collective-permute-start.8 = (bf16[3,2,64,512]{3,2,1,0:T(8,128)(2,1)}, bf16[3,2,64,512]{3,2,1,0:T(8,128)(2,1)}, u32[]{:S(2)}, u32[]{:S(2)}) collective-permute-start(bf16[3,2,64,512]{3,2,1,0:T(8,128)(2,1)} %collective-permute-done.5), channel_id=1, source_target_pairs={{0,192},{64,0},{128,64},{192,128},{256,448},{320,256},{384,320},{4... | collective-permute-start | bytes 1179656 | tf_op jit(solution)/shard_map/ppermute | solution.py:133
  34.1 30.1 %collective-permute-start.9 = (bf16[3,2,64,512]{3,2,1,0:T(8,128)(2,1)}, bf16[3,2,64,512]{3,2,1,0:T(8,128)(2,1)}, u32[]{:S(2)}, u32[]{:S(2)}) collective-permute-start(bf16[3,2,64,512]{3,2,1,0:T(8,128)(2,1)} %collective-permute-done.6), channel_id=1, source_target_pairs={{0,256},{64,320},{128,384},{192,448},{256,0},{320,64},{384,128},{4... | collective-permute-start | bytes 1179656 | tf_op jit(solution)/shard_map/ppermute | solution.py:133
  38.2 1.6 copy-start.1
  39.8 1.9 %slice-start = ((bf16[256,4,2,512]{3,2,1,0:T(2,128)(2,1)}), bf16[256,1,2,512]{3,2,1,0:T(2,128)(2,1)S(1)}, s32[]{:S(2)}) async-start(bf16[256,4,2,512]{3,2,1,0:T(2,128)(2,1)} %param.3), calls=%async_computation.3 | async-start | bytes 1048576 | tf_op jit(solution)/shard_map/slice | solution.py:197
  42.5 16.4 %copy-start.2 = (bf16[8,3,2,64,512]{4,3,2,0,1:T(8,128)(2,1)S(1)}, bf16[8,3,2,64,512]{4,3,2,0,1:T(8,128)(2,1)}, u32[]{:S(2)}) copy-start(bf16[8,3,2,64,512]{4,3,2,0,1:T(8,128)(2,1)} %copy-done.1) | copy-start | bytes 9437188
  43.5 41.0 %all-to-all-start.1 = ((bf16[16,4,1,2,8,256]{5,4,3,1,2,0:T(8,128)(2,1)}), bf16[16,4,1,2,8,256]{5,4,3,1,2,0:T(8,128)(2,1)}, u32[]{:S(2)}, u32[]{:S(2)}) async-start(bf16[16,4,1,2,8,256]{5,4,3,1,2,0:T(8,128)(2,1)} %bitcast.162), calls=%async_computation.1 | async-start | bytes 1048576 | tf_op jit(solution)/shard_map/all_to_all | solution.py:101
  59.9 5.4 %copy-start.3 = (bf16[1,256,3,2,512]{4,1,3,0,2:T(8,128)(2,1)S(1)}, bf16[1,256,3,2,512]{4,1,3,0,2:T(8,128)(2,1)}, u32[]{:S(2)}) copy-start(bf16[1,256,3,2,512]{4,1,3,0,2:T(8,128)(2,1)} %get-tuple-element.44) | copy-start | bytes 4718596
  59.9 5.4 %copy-start.4 = (bf16[1,256,3,2,512]{4,1,3,0,2:T(8,128)(2,1)S(1)}, bf16[1,256,3,2,512]{4,1,3,0,2:T(8,128)(2,1)}, u32[]{:S(2)}) copy-start(bf16[1,256,3,2,512]{4,1,3,0,2:T(8,128)(2,1)} %get-tuple-element.45) | copy-start | bytes 4718596
  68.5 26.3 %copy-start.5 = (f32[1024]{0:T(1024)S(1)}, f32[1024]{0:T(1024)}, u32[]{:S(2)}) copy-start(f32[1024]{0:T(1024)} %param.5) | copy-start | bytes 12292
  84.5 88.7 %all-to-all-start.2 = ((bf16[64,3,2,8,256]{4,3,2,1,0:T(8,128)(2,1)}), bf16[64,3,2,8,256]{4,3,2,1,0:T(8,128)(2,1)}, u32[]{:S(2)}, u32[]{:S(2)}) async-start(bf16[64,3,2,8,256]{4,3,2,1,0:T(8,128)(2,1)} %copy.91), calls=%async_computation.2 | async-start | bytes 3145728 | tf_op jit(solution)/shard_map/all_to_all | solution.py:95
  100.8 10.8 %collective-permute-start.2 = (bf16[16,1,2,8,256]{4,3,2,0,1:T(8,128)(2,1)S(1)}, bf16[16,1,2,8,256]{4,3,2,0,1:T(8,128)(2,1)S(1)}, u32[]{:S(2)}, u32[]{:S(2)}) collective-permute-start(bf16[16,1,2,8,256]{4,3,2,0,1:T(8,128)(2,1)S(1)} %get-tuple-element.34), channel_id=1, source_target_pairs={{0,3},{1,2},{2,1},{3,0},{4,7},{5,6},{6,5},{7,4},{8,11},{9,10},{10,... | collective-permute-start | bytes 393224 | tf_op jit(solution)/shard_map/ppermute | solution.py:123
  102.8 11.6 %collective-permute-start.1 = (bf16[16,1,2,8,256]{4,3,2,0,1:T(8,128)(2,1)S(1)}, bf16[16,1,2,8,256]{4,3,2,0,1:T(8,128)(2,1)S(1)}, u32[]{:S(2)}, u32[]{:S(2)}) collective-permute-start(bf16[16,1,2,8,256]{4,3,2,0,1:T(8,128)(2,1)S(1)} %get-tuple-element.32), channel_id=1, source_target_pairs={{0,2},{1,3},{2,0},{3,1},{4,6},{5,7},{6,4},{7,5},{8,10},{9,11},{10,... | collective-permute-start | bytes 393224 | tf_op jit(solution)/shard_map/ppermute | solution.py:123
  107.8 6.5 %collective-permute-start = (bf16[16,1,2,8,256]{4,3,2,0,1:T(8,128)(2,1)S(1)}, bf16[16,1,2,8,256]{4,3,2,0,1:T(8,128)(2,1)S(1)}, u32[]{:S(2)}, u32[]{:S(2)}) collective-permute-start(bf16[16,1,2,8,256]{4,3,2,0,1:T(8,128)(2,1)S(1)} %get-tuple-element.33), channel_id=1, source_target_pairs={{0,1},{1,0},{2,3},{3,2},{4,5},{5,4},{6,7},{7,6},{8,9},{9,8},{10,11... | collective-permute-start | bytes 393224 | tf_op jit(solution)/shard_map/ppermute | solution.py:123
  177.3 7.8 %collective-permute-start.10 = (f32[48,128]{1,0:T(8,128)S(1)}, f32[48,128]{1,0:T(8,128)S(1)}, u32[]{:S(2)}, u32[]{:S(2)}) collective-permute-start(f32[48,128]{1,0:T(8,128)S(1)} %bitcast.173), channel_id=1, source_target_pairs={{0,64},{64,128},{128,192},{192,256},{256,320},{320,384},{384,448},... | collective-permute-start | bytes 73736 | tf_op jit(solution)/shard_map/ppermute | solution.py:22

commit v4 on v3

--- a/solution.py
+++ b/solution.py
@@ -12,6 +12,7 @@
 K = 256
 FIRST_BIN = 32
 LANES = 128
+PARTS = 4
 PLANE = 4
 HEAD = 1
 
@@ -47,40 +48,52 @@
     return intersection
 
 
-def overlap_kernel(frames_ref, base_ref, out_ref):
+def overlap_kernel(frames_ref, base_ref, out_ref, done_ref, sems):
     beams, rows, hop_size = base_ref.shape
     lags = frames_ref.shape[2] // hop_size
     step, lanes = 32, out_ref.shape[1]
     halves = hop_size // lanes
-
-    def one_beam(b, carry):
-        for at in range(0, rows, step):
-            total = base_ref[b, pl.ds(at, step), :] + frames_ref[b, pl.ds(at, step), :hop_size]
-            for lag in range(1, lags):
-                columns = pl.ds(lag * hop_size, hop_size)
-                if at:
-                    total += frames_ref[b, pl.ds(at - lag, step), columns]
-                else:
-                    piece = pltpu.roll(frames_ref[b, pl.ds(0, step), columns], lag, 0)
-                    row = lax.broadcasted_iota(jnp.int32, piece.shape, 0)
-                    total += jnp.where(row < lag, 0.0, piece)
-            for half in range(halves):
-                rows_of = pl.ds((at * halves + half) * beams + b, step, stride=halves * beams)
-                out_ref[rows_of, :] = total[:, half * lanes : (half + 1) * lanes]
-        return carry
-
-    lax.fori_loop(0, beams, one_beam, 0)
+    part = rows // PARTS
+
+    def copy_of(index):
+        span = pl.ds(index * part * halves * beams, part * halves * beams)
+        return pltpu.make_async_copy(done_ref.at[span], out_ref.at[span], sems.at[index])
+
+    for index in range(PARTS):
+
+        def one_beam(b, carry):
+            for at in range(index * part, (index + 1) * part, step):
+                total = base_ref[b, pl.ds(at, step), :] + frames_ref[b, pl.ds(at, step), :hop_size]
+                for lag in range(1, lags):
+                    columns = pl.ds(lag * hop_size, hop_size)
+                    if at:
+                        total += frames_ref[b, pl.ds(at - lag, step), columns]
+                    else:
+                        piece = pltpu.roll(frames_ref[b, pl.ds(0, step), columns], lag, 0)
+                        row = lax.broadcasted_iota(jnp.int32, piece.shape, 0)
+                        total += jnp.where(row < lag, 0.0, piece)
+                for half in range(halves):
+                    rows_of = pl.ds((at * halves + half) * beams + b, step, stride=halves * beams)
+                    done_ref[rows_of, :] = total[:, half * lanes : (half + 1) * lanes]
+            return carry
+
+        lax.fori_loop(0, beams, one_beam, 0)
+        copy_of(index).start()
+    for index in range(PARTS):
+        copy_of(index).wait()
 
 
 def overlapped(frames, base):
     beams, rows, hop_size = base.shape
     lags = frames.shape[2] // hop_size
     whole = pl.BlockSpec(memory_space=pltpu.VMEM)
+    shape = (rows * hop_size // LANES * beams, LANES)
     return pl.pallas_call(
         overlap_kernel,
-        out_shape=jax.ShapeDtypeStruct((rows * hop_size // LANES * beams, LANES), jnp.float32),
+        out_shape=jax.ShapeDtypeStruct(shape, jnp.float32),
         in_specs=[whole, whole],
-        out_specs=whole,
+        out_specs=pl.BlockSpec(memory_space=pl.ANY),
+        scratch_shapes=[pltpu.VMEM(shape, jnp.float32), pltpu.SemaphoreType.DMA((PARTS,))],
         cost_estimate=pl.CostEstimate(
             flops=beams * lags * rows * hop_size,
             bytes_accessed=4 * beams * (lags + 2) * rows * hop_size,
@@ -134,12 +147,9 @@
 
 
 def own_row(block):
-    return (
-        across_tm(block, 1, 0),
-        across_tm(block, -1, 0),
-        across_tm(block, 0, 1),
-        across_tm(block, 2, 0),
-    )
+    across, far = across_tm(block, 0, 1), across_tm(block, 2, 0)
+    left, right = across_tm(block, 1, 0), across_tm(block, -1, 0)
+    return left, right, across, far
 
 
 def whole_table(block, left, right, across, far):
@@ -152,8 +162,9 @@
     y, x = me // ring, me % ring
     table = jnp.broadcast_to(block[None], (size,) + block.shape)
     for piece, dx, dy in (
-        (left, -1, 0), (right, 1, 0), (across, 0, 1), (far, 2, 0),
-        (across_left, -1, 1), (across_right, 1, 1), (across_far, 2, 1),
+        (across, 0, 1), (far, 2, 0), (across_left, -1, 1),
+        (left, -1, 0), (right, 1, 0),
+        (across_right, 1, 1), (across_far, 2, 1),
     ):
         at = ((y + dy) % 2) * ring + (x + dx + ring) % ring
         table = lax.dynamic_update_slice(table, piece[None], (at,) + (0,) * block.ndim)
@@ -193,11 +204,13 @@
     size = lax.axis_size("tm")
     head = blocks[:HEAD]
     head = exchanged(jnp.broadcast_to(head[None], (size,) + head.shape), "tm")
-    row = own_row(blocks[HEAD:])
+    left, right, across, far = own_row(blocks[HEAD:])
     message = beam_form_of_pairs(samples[:, :HEAD], head)
     head_spectra = along_z(in_planes(message))
-    samples, row, block, _ = lax.optimization_barrier((samples, row, blocks[HEAD:], message))
-    rest = whole_table(block, *row)
+    samples, across, far, block, _ = lax.optimization_barrier(
+        (samples, across, far, blocks[HEAD:], message)
+    )
+    rest = whole_table(block, left, right, across, far)
     rest_message = beam_form(with_quadrature(samples[:, HEAD:]), rest)
     rest_spectra = exchanged(rest_message, "band")
     head_spectra = within_plane(head_spectra).reshape(message.shape)

time: 187 us -> 184 us (0.984)
    ppermute x7, waiting for transfers between devices: 3.94 us -> 0.02 us  [across_tm(): return lax.ppermute(array, 'tm', route)]
  transfers between devices with their start and end apart: 14 -> 14, of which waited for: 6 -> 4; matrix products, arithmetic and copies ran while one was open for 15% -> 15% of each run, Pallas kernels for 1% -> 1%
where the time goes in v4:
time: 184 us; the launch traced here: 183 us
  waiting for transfers between devices  78.3 us (43%)
  starting transfers between devices  65.9 us (36%)
  local copies, waits for them, and re-layouts  18.1 us (10%)
  other arithmetic  10.4 us (6%)
  matrix products  7.73 us (4%)
  Pallas kernels  2.15 us (1%)
    all_to_all x2, waiting for transfers between devices, exchanged(): return lax.all_to_all(block, axis, split_axis=0, concat_axis=0, tiled=True)  55.2 us
    ppermute x7, starting transfers between devices, across_tm(): return lax.ppermute(array, 'tm', route)  23.7 us
    all_to_all x1, waiting for transfers between devices, along_z(): lax.all_to_all(block, 'band', split_axis=0, concat_axis=0, tiled=True, ax...  16.5 us
    all_to_all x2, starting transfers between devices, exchanged(): return lax.all_to_all(block, axis, split_axis=0, concat_axis=0, tiled=True)  15.7 us
    all_to_all x1, starting transfers between devices, along_z(): lax.all_to_all(block, 'band', split_axis=0, concat_axis=0, tiled=True, ax...  15.4 us
    ppermute x3, starting transfers between devices, within_plane(): pieces[step] = lax.ppermute(pieces[step], 'band', route)  9.27 us
    dynamic_update_slice x7, local copies, waits for them, and re-layouts, whole_table(): lax.dynamic_update_slice(table, piece[None], (at,) + (0,) * block.ndim)  7.35 us
    dot_general x2, matrix products, synthesize(): jnp.einsum('skcbf,skcm->bfm', spectra, part, preferred_element_type=jnp.f...  5.16 us
  transfers between devices with their start and end apart: 14, of which 4 were waited for; matrix products, arithmetic and copies ran while one was open for 15% of the time, Pallas kernels for 1%

profile of v4, /device:TPU:24, one launch (start us, length us, event | category | flops | bytes accessed | tf_op | source)
XLA Modules:
  0.0 183.3 jit_solution(6260547976683658465)
XLA Ops:
  1.0 2.7 %collective-permute-start.3 = (bf16[3,2,64,512]{3,2,1,0:T(8,128)(2,1)S(1)}, bf16[3,2,64,512]{3,2,1,0:T(8,128)(2,1)}, u32[]{:S(2)}, u32[]{:S(2)}) collective-permute-start(bf16[3,2,64,512]{3,2,1,0:T(8,128)(2,1)S(1)} %slice.117), channel_id=1, source_target_pairs={{0,256},{64,320},{128,384},{192,448},{256,0},{320,64},{384,128},{4... | collective-permute-start | bytes 1179656 | tf_op jit(solution)/shard_map/ppermute | solution.py:146
  3.7 4.9 %collective-permute-start.4 = (bf16[3,2,64,512]{3,2,1,0:T(8,128)(2,1)S(1)}, bf16[3,2,64,512]{3,2,1,0:T(8,128)(2,1)}, u32[]{:S(2)}, u32[]{:S(2)}) collective-permute-start(bf16[3,2,64,512]{3,2,1,0:T(8,128)(2,1)S(1)} %slice.117), channel_id=1, source_target_pairs={{0,128},{64,192},{128,0},{192,64},{256,384},{320,448},{384,256},{4... | collective-permute-start | bytes 1179656 | tf_op jit(solution)/shard_map/ppermute | solution.py:146
  9.6 1.1 broadcast_in_dim.39
  10.7 4.8 %all-to-all-start = ((bf16[8,1,2,64,512]{4,3,2,1,0:T(8,128)(2,1)}), bf16[8,1,2,64,512]{4,3,2,1,0:T(8,128)(2,1)S(1)}, u32[]{:S(2)}, u32[]{:S(2)}) async-start(bf16[8,1,2,64,512]{4,3,2,1,0:T(8,128)(2,1)} %broadcast_in_dim.39), calls=%async_computation | async-start | bytes 2097152 | tf_op jit(solution)/shard_map/all_to_all | solution.py:108
  15.4 3.4 %collective-permute-start.6 = (bf16[3,2,64,512]{3,2,1,0:T(8,128)(2,1)S(1)}, bf16[3,2,64,512]{3,2,1,0:T(8,128)(2,1)}, u32[]{:S(2)}, u32[]{:S(2)}) collective-permute-start(bf16[3,2,64,512]{3,2,1,0:T(8,128)(2,1)S(1)} %slice.117), channel_id=1, source_target_pairs={{0,64},{64,128},{128,192},{192,0},{256,320},{320,384},{384,448},{4... | collective-permute-start | bytes 1179656 | tf_op jit(solution)/shard_map/ppermute | solution.py:146
  18.8 3.7 %collective-permute-start.7 = (bf16[3,2,64,512]{3,2,1,0:T(8,128)(2,1)S(1)}, bf16[3,2,64,512]{3,2,1,0:T(8,128)(2,1)}, u32[]{:S(2)}, u32[]{:S(2)}) collective-permute-start(bf16[3,2,64,512]{3,2,1,0:T(8,128)(2,1)S(1)} %slice.117), channel_id=1, source_target_pairs={{0,192},{64,0},{128,64},{192,128},{256,448},{320,256},{384,320},{4... | collective-permute-start | bytes 1179656 | tf_op jit(solution)/shard_map/ppermute | solution.py:146
  22.6 2.2 %collective-permute-start.5 = (bf16[3,2,64,512]{3,2,1,0:T(8,128)(2,1)}, bf16[3,2,64,512]{3,2,1,0:T(8,128)(2,1)}, u32[]{:S(2)}, u32[]{:S(2)}) collective-permute-start(bf16[3,2,64,512]{3,2,1,0:T(8,128)(2,1)} %collective-permute-done.3), channel_id=1, source_target_pairs={{0,64},{64,128},{128,192},{192,0},{256,320},{320,384},{384,448},{4... | collective-permute-start | bytes 1179656 | tf_op jit(solution)/shard_map/ppermute | solution.py:146
  24.8 4.9 %collective-permute-start.8 = (bf16[3,2,64,512]{3,2,1,0:T(8,128)(2,1)}, bf16[3,2,64,512]{3,2,1,0:T(8,128)(2,1)}, u32[]{:S(2)}, u32[]{:S(2)}) collective-permute-start(bf16[3,2,64,512]{3,2,1,0:T(8,128)(2,1)} %collective-permute-done.3), channel_id=1, source_target_pairs={{0,192},{64,0},{128,64},{192,128},{256,448},{320,256},{384,320},{4... | collective-permute-start | bytes 1179656 | tf_op jit(solution)/shard_map/ppermute | solution.py:146
  30.4 2.0 %collective-permute-start.9 = (bf16[3,2,64,512]{3,2,1,0:T(8,128)(2,1)}, bf16[3,2,64,512]{3,2,1,0:T(8,128)(2,1)}, u32[]{:S(2)}, u32[]{:S(2)}) collective-permute-start(bf16[3,2,64,512]{3,2,1,0:T(8,128)(2,1)} %collective-permute-done.4), channel_id=1, source_target_pairs={{0,256},{64,320},{128,384},{192,448},{256,0},{320,64},{384,128},{4... | collective-permute-start | bytes 1179656 | tf_op jit(solution)/shard_map/ppermute | solution.py:146
  32.8 1.0 bitcast_dynamic-update-slice_fusion.6
  33.9 1.5 copy-done.1
  35.5 1.9 %slice_bitcast_fusion.4 = (bf16[1,256,3,2,512]{4,1,3,0,2:T(8,128)(2,1)}, bf16[1,256,3,2,512]{4,1,3,0,2:T(8,128)(2,1)}) fusion(bf16[256,4,2,512]{3,0,2,1:T(8,128)(2,1)S(1)} %copy.87, bf16[256,3,1,512]{3,0,2,1:T(8,128)(2,1)S(1)} %get-tuple-element.24, bf16[256,3,1,512]{3,0,2,1:T(8,128)(2,1)S(1)} %get-tuple-element.23), kind=kLoop, calls=%fused_computation.14 | loop fusion | flops 786432 | bytes 6291456 | tf_op jit(solution)/shard_map/stack | solution.py:175
  39.1 15.4 %all-to-all-start.1 = ((bf16[16,4,1,2,8,256]{5,4,3,1,2,0:T(8,128)(2,1)}), bf16[16,4,1,2,8,256]{5,4,3,1,2,0:T(8,128)(2,1)}, u32[]{:S(2)}, u32[]{:S(2)}) async-start(bf16[16,4,1,2,8,256]{5,4,3,1,2,0:T(8,128)(2,1)} %bitcast.162), calls=%async_computation.1 | async-start | bytes 1048576 | tf_op jit(solution)/shard_map/all_to_all | solution.py:114
  54.5 1.0 bitcast_dynamic-update-slice_fusion.5
  55.6 1.2 bitcast_dynamic-update-slice_fusion.4
  61.0 1.8 fusion.7
  62.9 1.3 copy.91
  64.2 16.5 %all-to-all-done.1 = bf16[16,4,1,2,8,256]{5,4,3,1,2,0:T(8,128)(2,1)} async-done(((bf16[16,4,1,2,8,256]{5,4,3,1,2,0:T(8,128)(2,1)}), bf16[16,4,1,2,8,256]{5,4,3,1,2,0:T(8,128)(2,1)}, u32[]{:S(2)}, u32[]{:S(2)}) %all-to-all-start.1) | async-done | bytes 524320 | tf_op jit(solution)/shard_map/all_to_all | solution.py:114
  80.7 10.9 %all-to-all-start.2 = ((bf16[64,3,2,8,256]{4,3,2,1,0:T(8,128)(2,1)}), bf16[64,3,2,8,256]{4,3,2,1,0:T(8,128)(2,1)}, u32[]{:S(2)}, u32[]{:S(2)}) async-start(bf16[64,3,2,8,256]{4,3,2,1,0:T(8,128)(2,1)} %copy.91), calls=%async_computation.2 | async-start | bytes 3145728 | tf_op jit(solution)/shard_map/all_to_all | solution.py:108
  91.7 4.6 %multiply_convert_fusion.1 = (bf16[64,4,1,1024]{3,0,1,2:T(8,128)(2,1)S(1)}, bf16[64,4,1,1024]{3,0,1,2:T(8,128)(2,1)S(1)}) fusion(f32[1024]{0:T(1024)S(1)} %broadcast_multiply_fusion, s32[64,4]{0,1:T(4,128)S(1)} %add_add_fusion), kind=kLoop, calls=%fused_computation.26 | loop fusion | flops 4980736 | bytes 1053696 | tf_op jit(solution)/shard_map/convert
  96.4 1.1 dynamic-slice_bitcast_fusion.3
  97.6 2.0 %collective-permute-start.2 = (bf16[16,1,2,8,256]{4,3,2,0,1:T(8,128)(2,1)S(1)}, bf16[16,1,2,8,256]{4,3,2,0,1:T(8,128)(2,1)S(1)}, u32[]{:S(2)}, u32[]{:S(2)}) collective-permute-start(bf16[16,1,2,8,256]{4,3,2,0,1:T(8,128)(2,1)S(1)} %get-tuple-element.30), channel_id=1, source_target_pairs={{0,3},{1,2},{2,1},{3,0},{4,7},{5,6},{6,5},{7,4},{8,11},{9,10},{10,... | collective-permute-start | bytes 393224 | tf_op jit(solution)/shard_map/ppermute | solution.py:136
  99.6 5.0 %collective-permute-start.1 = (bf16[16,1,2,8,256]{4,3,2,0,1:T(8,128)(2,1)S(1)}, bf16[16,1,2,8,256]{4,3,2,0,1:T(8,128)(2,1)S(1)}, u32[]{:S(2)}, u32[]{:S(2)}) collective-permute-start(bf16[16,1,2,8,256]{4,3,2,0,1:T(8,128)(2,1)S(1)} %get-tuple-element.28), channel_id=1, source_target_pairs={{0,2},{1,3},{2,0},{3,1},{4,6},{5,7},{6,4},{7,5},{8,10},{9,11},{10,... | collective-permute-start | bytes 393224 | tf_op jit(solution)/shard_map/ppermute | solution.py:136
  104.7 2.2 %collective-permute-start = (bf16[16,1,2,8,256]{4,3,2,0,1:T(8,128)(2,1)S(1)}, bf16[16,1,2,8,256]{4,3,2,0,1:T(8,128)(2,1)S(1)}, u32[]{:S(2)}, u32[]{:S(2)}) collective-permute-start(bf16[16,1,2,8,256]{4,3,2,0,1:T(8,128)(2,1)S(1)} %get-tuple-element.29), channel_id=1, source_target_pairs={{0,1},{1,0},{2,3},{3,2},{4,5},{5,4},{6,7},{7,6},{8,9},{9,8},{10,11... | collective-permute-start | bytes 393224 | tf_op jit(solution)/shard_map/ppermute | solution.py:136
  108.4 2.8 %collective-permute-done.1 = bf16[16,1,2,8,256]{4,3,2,0,1:T(8,128)(2,1)S(1)} collective-permute-done((bf16[16,1,2,8,256]{4,3,2,0,1:T(8,128)(2,1)S(1)}, bf16[16,1,2,8,256]{4,3,2,0,1:T(8,128)(2,1)S(1)}, u32[]{:S(2)}, u32[]{:S(2)}) %collective-permute-start.1) | collective-permute-done | bytes 131104 | tf_op jit(solution)/shard_map/ppermute | solution.py:136
  111.8 1.3 convolution_bitcast_fusion.1
  114.8 55.2 %all-to-all-done.2 = bf16[64,3,2,8,256]{4,3,2,1,0:T(8,128)(2,1)} async-done(((bf16[64,3,2,8,256]{4,3,2,1,0:T(8,128)(2,1)}), bf16[64,3,2,8,256]{4,3,2,1,0:T(8,128)(2,1)}, u32[]{:S(2)}, u32[]{:S(2)}) %all-to-all-start.2) | async-done | bytes 1572896 | tf_op jit(solution)/shard_map/all_to_all | solution.py:108
  170.1 3.9 %convolution_bitcast_fusion.frames_ref = f32[8,256,1024]{2,1,0:T(8,128)S(1)} fusion(bf16[64,3,2,8,256]{4,3,2,1,0:T(8,128)(2,1)} %all-to-all-done.2, bf16[64,4,1,1024]{3,0,1,2:T(8,128)(2,1)S(1)} %get-tuple-element.39, bf16[64,4,1,1024]{3,0,1,2:T(8,128)(2,1)S(1)} %get-tuple-element.38), kind=kOutput, calls=%fused_computation | convolution fusion | flops 1611005952 | bytes 11010048 | tf_op jit(solution)/shard_map/skcbf,skcm->bfm/dot_general | solution.py:226
  174.1 1.9 %collective-permute-start.10 = (f32[48,128]{1,0:T(8,128)S(1)}, f32[48,128]{1,0:T(8,128)S(1)}, u32[]{:S(2)}, u32[]{:S(2)}) collective-permute-start(f32[48,128]{1,0:T(8,128)S(1)} %bitcast.173), channel_id=1, source_target_pairs={{0,64},{64,128},{128,192},{192,256},{256,320},{320,384},{384,448},... | collective-permute-start | bytes 73736 | tf_op jit(solution)/shard_map/ppermute | solution.py:23
  176.0 2.1 %overlap.1 = f32[4096,128]{1,0:T(8,128)} custom-call(f32[8,256,1024]{2,1,0:T(8,128)S(1)} %convolution_bitcast_fusion.frames_ref, f32[8,256,256]{2,1,0:T(8,128)S(1)} %slice.116.base_ref), custom_call_target="tpu_custom_call" | custom-call | flops 2097152 | bytes 12582912 | tf_op jit(solution)/shard_map/overlap/pallas_call | solution.py:91
  178.2 3.7 %collective-permute-done.10 = f32[48,128]{1,0:T(8,128)S(1)} collective-permute-done((f32[48,128]{1,0:T(8,128)S(1)}, f32[48,128]{1,0:T(8,128)S(1)}, u32[]{:S(2)}, u32[]{:S(2)}) %collective-permute-start.10) | collective-permute-done | bytes 24608 | tf_op jit(solution)/shard_map/ppermute | solution.py:23
  181.9 1.4 fusion.23
  (55 shorter events, 13.1 us)
Async XLA Ops:
  1.0 21.6 %collective-permute-start.3 = (bf16[3,2,64,512]{3,2,1,0:T(8,128)(2,1)S(1)}, bf16[3,2,64,512]{3,2,1,0:T(8,128)(2,1)}, u32[]{:S(2)}, u32[]{:S(2)}) collective-permute-start(bf16[3,2,64,512]{3,2,1,0:T(8,128)(2,1)S(1)} %slice.117), channel_id=1, source_target_pairs={{0,256},{64,320},{128,384},{192,448},{256,0},{320,64},{384,128},{4... | collective-permute-start | bytes 1179656 | tf_op jit(solution)/shard_map/ppermute | solution.py:146
  3.7 18.9 %collective-permute-start.4 = (bf16[3,2,64,512]{3,2,1,0:T(8,128)(2,1)S(1)}, bf16[3,2,64,512]{3,2,1,0:T(8,128)(2,1)}, u32[]{:S(2)}, u32[]{:S(2)}) collective-permute-start(bf16[3,2,64,512]{3,2,1,0:T(8,128)(2,1)S(1)} %slice.117), channel_id=1, source_target_pairs={{0,128},{64,192},{128,0},{192,64},{256,384},{320,448},{384,256},{4... | collective-permute-start | bytes 1179656 | tf_op jit(solution)/shard_map/ppermute | solution.py:146
  9.5 20.2 %copy-start = (bf16[256,4,2,512]{3,2,1,0:T(2,128)(2,1)S(1)}, bf16[256,4,2,512]{3,2,1,0:T(2,128)(2,1)}, u32[]{:S(2)}) copy-start(bf16[256,4,2,512]{3,2,1,0:T(2,128)(2,1)} %param.3) | copy-start | bytes 6291460
  10.7 26.7 %all-to-all-start = ((bf16[8,1,2,64,512]{4,3,2,1,0:T(8,128)(2,1)}), bf16[8,1,2,64,512]{4,3,2,1,0:T(8,128)(2,1)S(1)}, u32[]{:S(2)}, u32[]{:S(2)}) async-start(bf16[8,1,2,64,512]{4,3,2,1,0:T(8,128)(2,1)} %broadcast_in_dim.39), calls=%async_computation | async-start | bytes 2097152 | tf_op jit(solution)/shard_map/all_to_all | solution.py:108
  15.4 41.4 %collective-permute-start.6 = (bf16[3,2,64,512]{3,2,1,0:T(8,128)(2,1)S(1)}, bf16[3,2,64,512]{3,2,1,0:T(8,128)(2,1)}, u32[]{:S(2)}, u32[]{:S(2)}) collective-permute-start(bf16[3,2,64,512]{3,2,1,0:T(8,128)(2,1)S(1)} %slice.117), channel_id=1, source_target_pairs={{0,64},{64,128},{128,192},{192,0},{256,320},{320,384},{384,448},{4... | collective-permute-start | bytes 1179656 | tf_op jit(solution)/shard_map/ppermute | solution.py:146
  18.8 39.0 %collective-permute-start.7 = (bf16[3,2,64,512]{3,2,1,0:T(8,128)(2,1)S(1)}, bf16[3,2,64,512]{3,2,1,0:T(8,128)(2,1)}, u32[]{:S(2)}, u32[]{:S(2)}) collective-permute-start(bf16[3,2,64,512]{3,2,1,0:T(8,128)(2,1)S(1)} %slice.117), channel_id=1, source_target_pairs={{0,192},{64,0},{128,64},{192,128},{256,448},{320,256},{384,320},{4... | collective-permute-start | bytes 1179656 | tf_op jit(solution)/shard_map/ppermute | solution.py:146
  22.6 33.0 %collective-permute-start.5 = (bf16[3,2,64,512]{3,2,1,0:T(8,128)(2,1)}, bf16[3,2,64,512]{3,2,1,0:T(8,128)(2,1)}, u32[]{:S(2)}, u32[]{:S(2)}) collective-permute-start(bf16[3,2,64,512]{3,2,1,0:T(8,128)(2,1)} %collective-permute-done.3), channel_id=1, source_target_pairs={{0,64},{64,128},{128,192},{192,0},{256,320},{320,384},{384,448},{4... | collective-permute-start | bytes 1179656 | tf_op jit(solution)/shard_map/ppermute | solution.py:146
  24.8 34.1 %collective-permute-start.8 = (bf16[3,2,64,512]{3,2,1,0:T(8,128)(2,1)}, bf16[3,2,64,512]{3,2,1,0:T(8,128)(2,1)}, u32[]{:S(2)}, u32[]{:S(2)}) collective-permute-start(bf16[3,2,64,512]{3,2,1,0:T(8,128)(2,1)} %collective-permute-done.3), channel_id=1, source_target_pairs={{0,192},{64,0},{128,64},{192,128},{256,448},{320,256},{384,320},{4... | collective-permute-start | bytes 1179656 | tf_op jit(solution)/shard_map/ppermute | solution.py:146
  30.4 29.5 %collective-permute-start.9 = (bf16[3,2,64,512]{3,2,1,0:T(8,128)(2,1)}, bf16[3,2,64,512]{3,2,1,0:T(8,128)(2,1)}, u32[]{:S(2)}, u32[]{:S(2)}) collective-permute-start(bf16[3,2,64,512]{3,2,1,0:T(8,128)(2,1)} %collective-permute-done.4), channel_id=1, source_target_pairs={{0,256},{64,320},{128,384},{192,448},{256,0},{320,64},{384,128},{4... | collective-permute-start | bytes 1179656 | tf_op jit(solution)/shard_map/ppermute | solution.py:146
  33.8 1.6 copy-start.1
  35.5 1.9 %slice-start = ((bf16[256,4,2,512]{3,2,1,0:T(2,128)(2,1)}), bf16[256,1,2,512]{3,2,1,0:T(2,128)(2,1)S(1)}, s32[]{:S(2)}) async-start(bf16[256,4,2,512]{3,2,1,0:T(2,128)(2,1)} %param.3), calls=%async_computation.3 | async-start | bytes 1048576 | tf_op jit(solution)/shard_map/slice | solution.py:208
  38.1 16.4 %copy-start.2 = (bf16[8,3,2,64,512]{4,3,2,0,1:T(8,128)(2,1)S(1)}, bf16[8,3,2,64,512]{4,3,2,0,1:T(8,128)(2,1)}, u32[]{:S(2)}) copy-start(bf16[8,3,2,64,512]{4,3,2,0,1:T(8,128)(2,1)} %copy-done.1) | copy-start | bytes 9437188
  39.1 41.5 %all-to-all-start.1 = ((bf16[16,4,1,2,8,256]{5,4,3,1,2,0:T(8,128)(2,1)}), bf16[16,4,1,2,8,256]{5,4,3,1,2,0:T(8,128)(2,1)}, u32[]{:S(2)}, u32[]{:S(2)}) async-start(bf16[16,4,1,2,8,256]{5,4,3,1,2,0:T(8,128)(2,1)} %bitcast.162), calls=%async_computation.1 | async-start | bytes 1048576 | tf_op jit(solution)/shard_map/all_to_all | solution.py:114
  55.6 5.4 %copy-start.3 = (bf16[1,256,3,2,512]{4,1,3,0,2:T(8,128)(2,1)S(1)}, bf16[1,256,3,2,512]{4,1,3,0,2:T(8,128)(2,1)}, u32[]{:S(2)}) copy-start(bf16[1,256,3,2,512]{4,1,3,0,2:T(8,128)(2,1)} %get-tuple-element.40) | copy-start | bytes 4718596
  55.6 5.4 %copy-start.4 = (bf16[1,256,3,2,512]{4,1,3,0,2:T(8,128)(2,1)S(1)}, bf16[1,256,3,2,512]{4,1,3,0,2:T(8,128)(2,1)}, u32[]{:S(2)}) copy-start(bf16[1,256,3,2,512]{4,1,3,0,2:T(8,128)(2,1)} %get-tuple-element.41) | copy-start | bytes 4718596
  64.2 27.4 %copy-start.5 = (f32[1024]{0:T(1024)S(1)}, f32[1024]{0:T(1024)}, u32[]{:S(2)}) copy-start(f32[1024]{0:T(1024)} %param.5) | copy-start | bytes 12292
  80.7 89.4 %all-to-all-start.2 = ((bf16[64,3,2,8,256]{4,3,2,1,0:T(8,128)(2,1)}), bf16[64,3,2,8,256]{4,3,2,1,0:T(8,128)(2,1)}, u32[]{:S(2)}, u32[]{:S(2)}) async-start(bf16[64,3,2,8,256]{4,3,2,1,0:T(8,128)(2,1)} %copy.91), calls=%async_computation.2 | async-start | bytes 3145728 | tf_op jit(solution)/shard_map/all_to_all | solution.py:108
  97.6 10.8 %collective-permute-start.2 = (bf16[16,1,2,8,256]{4,3,2,0,1:T(8,128)(2,1)S(1)}, bf16[16,1,2,8,256]{4,3,2,0,1:T(8,128)(2,1)S(1)}, u32[]{:S(2)}, u32[]{:S(2)}) collective-permute-start(bf16[16,1,2,8,256]{4,3,2,0,1:T(8,128)(2,1)S(1)} %get-tuple-element.30), channel_id=1, source_target_pairs={{0,3},{1,2},{2,1},{3,0},{4,7},{5,6},{6,5},{7,4},{8,11},{9,10},{10,... | collective-permute-start | bytes 393224 | tf_op jit(solution)/shard_map/ppermute | solution.py:136
  99.6 11.6 %collective-permute-start.1 = (bf16[16,1,2,8,256]{4,3,2,0,1:T(8,128)(2,1)S(1)}, bf16[16,1,2,8,256]{4,3,2,0,1:T(8,128)(2,1)S(1)}, u32[]{:S(2)}, u32[]{:S(2)}) collective-permute-start(bf16[16,1,2,8,256]{4,3,2,0,1:T(8,128)(2,1)S(1)} %get-tuple-element.28), channel_id=1, source_target_pairs={{0,2},{1,3},{2,0},{3,1},{4,6},{5,7},{6,4},{7,5},{8,10},{9,11},{10,... | collective-permute-start | bytes 393224 | tf_op jit(solution)/shard_map/ppermute | solution.py:136
  104.7 6.5 %collective-permute-start = (bf16[16,1,2,8,256]{4,3,2,0,1:T(8,128)(2,1)S(1)}, bf16[16,1,2,8,256]{4,3,2,0,1:T(8,128)(2,1)S(1)}, u32[]{:S(2)}, u32[]{:S(2)}) collective-permute-start(bf16[16,1,2,8,256]{4,3,2,0,1:T(8,128)(2,1)S(1)} %get-tuple-element.29), channel_id=1, source_target_pairs={{0,1},{1,0},{2,3},{3,2},{4,5},{5,4},{6,7},{7,6},{8,9},{9,8},{10,11... | collective-permute-start | bytes 393224 | tf_op jit(solution)/shard_map/ppermute | solution.py:136
  174.1 7.8 %collective-permute-start.10 = (f32[48,128]{1,0:T(8,128)S(1)}, f32[48,128]{1,0:T(8,128)S(1)}, u32[]{:S(2)}, u32[]{:S(2)}) collective-permute-start(f32[48,128]{1,0:T(8,128)S(1)} %bitcast.173), channel_id=1, source_target_pairs={{0,64},{64,128},{128,192},{192,256},{256,320},{320,384},{384,448},... | collective-permute-start | bytes 73736 | tf_op jit(solution)/shard_map/ppermute | solution.py:23

commit v5 on v4

--- a/solution.py
+++ b/solution.py
@@ -147,14 +147,16 @@
 
 
 def own_row(block):
-    across, far = across_tm(block, 0, 1), across_tm(block, 2, 0)
+    across = across_tm(block, 0, 1)
     left, right = across_tm(block, 1, 0), across_tm(block, -1, 0)
+    far = across_tm(block, 2, 0)
     return left, right, across, far
 
 
 def whole_table(block, left, right, across, far):
     across_left = across_tm(across, 1, 0)
     across_right = across_tm(across, -1, 0)
+    far, block = lax.optimization_barrier((far, block))
     across_far = across_tm(far, 0, 1)
     size = lax.axis_size("tm")
     ring = size // 2
@@ -207,8 +209,8 @@
     left, right, across, far = own_row(blocks[HEAD:])
     message = beam_form_of_pairs(samples[:, :HEAD], head)
     head_spectra = along_z(in_planes(message))
-    samples, across, far, block, _ = lax.optimization_barrier(
-        (samples, across, far, blocks[HEAD:], message)
+    samples, across, block, _ = lax.optimization_barrier(
+        (samples, across, blocks[HEAD:], message)
     )
     rest = whole_table(block, left, right, across, far)
     rest_message = beam_form(with_quadrature(samples[:, HEAD:]), rest)

time: 184 us -> 184 us (level)
  no operation moved by 1% of the time
where the time goes in v5:
time: 184 us; the launch traced here: 183 us
  waiting for transfers between devices  78.2 us (42%)
  starting transfers between devices  65.9 us (36%)
  local copies, waits for them, and re-layouts  18.1 us (10%)
  other arithmetic  10.4 us (6%)
  matrix products  7.73 us (4%)
  Pallas kernels  2.15 us (1%)
    all_to_all x2, waiting for transfers between devices, exchanged(): return lax.all_to_all(block, axis, split_axis=0, concat_axis=0, tiled=True)  55.2 us
    ppermute x7, starting transfers between devices, across_tm(): return lax.ppermute(array, 'tm', route)  23.7 us
    all_to_all x1, waiting for transfers between devices, along_z(): lax.all_to_all(block, 'band', split_axis=0, concat_axis=0, tiled=True, ax...  16.5 us
    all_to_all x2, starting transfers between devices, exchanged(): return lax.all_to_all(block, axis, split_axis=0, concat_axis=0, tiled=True)  15.7 us
    all_to_all x1, starting transfers between devices, along_z(): lax.all_to_all(block, 'band', split_axis=0, concat_axis=0, tiled=True, ax...  15.4 us
    ppermute x3, starting transfers between devices, within_plane(): pieces[step] = lax.ppermute(pieces[step], 'band', route)  9.27 us
    dynamic_update_slice x7, local copies, waits for them, and re-layouts, whole_table(): lax.dynamic_update_slice(table, piece[None], (at,) + (0,) * block.ndim)  7.35 us
    dot_general x2, matrix products, synthesize(): jnp.einsum('skcbf,skcm->bfm', spectra, part, preferred_element_type=jnp.f...  5.16 us
  transfers between devices with their start and end apart: 14, of which 4 were waited for; matrix products, arithmetic and copies ran while one was open for 15% of the time, Pallas kernels for 1%

profile of v5, /device:TPU:24, one launch (start us, length us, event | category | flops | bytes accessed | tf_op | source)
XLA Modules:
  0.0 183.3 jit_solution(17997641334200305317)
XLA Ops:
  1.0 2.7 %collective-permute-start.4 = (bf16[3,2,64,512]{3,2,1,0:T(8,128)(2,1)S(1)}, bf16[3,2,64,512]{3,2,1,0:T(8,128)(2,1)}, u32[]{:S(2)}, u32[]{:S(2)}) collective-permute-start(bf16[3,2,64,512]{3,2,1,0:T(8,128)(2,1)S(1)} %slice.117), channel_id=1, source_target_pairs={{0,256},{64,320},{128,384},{192,448},{256,0},{320,64},{384,128},{4... | collective-permute-start | bytes 1179656 | tf_op jit(solution)/shard_map/ppermute | solution.py:146
  3.7 4.9 %collective-permute-start.3 = (bf16[3,2,64,512]{3,2,1,0:T(8,128)(2,1)S(1)}, bf16[3,2,64,512]{3,2,1,0:T(8,128)(2,1)}, u32[]{:S(2)}, u32[]{:S(2)}) collective-permute-start(bf16[3,2,64,512]{3,2,1,0:T(8,128)(2,1)S(1)} %slice.117), channel_id=1, source_target_pairs={{0,128},{64,192},{128,0},{192,64},{256,384},{320,448},{384,256},{4... | collective-permute-start | bytes 1179656 | tf_op jit(solution)/shard_map/ppermute | solution.py:146
  9.6 1.1 broadcast_in_dim.39
  10.7 4.8 %all-to-all-start = ((bf16[8,1,2,64,512]{4,3,2,1,0:T(8,128)(2,1)}), bf16[8,1,2,64,512]{4,3,2,1,0:T(8,128)(2,1)S(1)}, u32[]{:S(2)}, u32[]{:S(2)}) async-start(bf16[8,1,2,64,512]{4,3,2,1,0:T(8,128)(2,1)} %broadcast_in_dim.39), calls=%async_computation | async-start | bytes 2097152 | tf_op jit(solution)/shard_map/all_to_all | solution.py:108
  15.4 3.4 %collective-permute-start.6 = (bf16[3,2,64,512]{3,2,1,0:T(8,128)(2,1)S(1)}, bf16[3,2,64,512]{3,2,1,0:T(8,128)(2,1)}, u32[]{:S(2)}, u32[]{:S(2)}) collective-permute-start(bf16[3,2,64,512]{3,2,1,0:T(8,128)(2,1)S(1)} %slice.117), channel_id=1, source_target_pairs={{0,64},{64,128},{128,192},{192,0},{256,320},{320,384},{384,448},{4... | collective-permute-start | bytes 1179656 | tf_op jit(solution)/shard_map/ppermute | solution.py:146
  18.8 3.7 %collective-permute-start.7 = (bf16[3,2,64,512]{3,2,1,0:T(8,128)(2,1)S(1)}, bf16[3,2,64,512]{3,2,1,0:T(8,128)(2,1)}, u32[]{:S(2)}, u32[]{:S(2)}) collective-permute-start(bf16[3,2,64,512]{3,2,1,0:T(8,128)(2,1)S(1)} %slice.117), channel_id=1, source_target_pairs={{0,192},{64,0},{128,64},{192,128},{256,448},{320,256},{384,320},{4... | collective-permute-start | bytes 1179656 | tf_op jit(solution)/shard_map/ppermute | solution.py:146
  22.6 2.2 %collective-permute-start.5 = (bf16[3,2,64,512]{3,2,1,0:T(8,128)(2,1)}, bf16[3,2,64,512]{3,2,1,0:T(8,128)(2,1)}, u32[]{:S(2)}, u32[]{:S(2)}) collective-permute-start(bf16[3,2,64,512]{3,2,1,0:T(8,128)(2,1)} %collective-permute-done.4), channel_id=1, source_target_pairs={{0,64},{64,128},{128,192},{192,0},{256,320},{320,384},{384,448},{4... | collective-permute-start | bytes 1179656 | tf_op jit(solution)/shard_map/ppermute | solution.py:146
  24.8 4.9 %collective-permute-start.8 = (bf16[3,2,64,512]{3,2,1,0:T(8,128)(2,1)}, bf16[3,2,64,512]{3,2,1,0:T(8,128)(2,1)}, u32[]{:S(2)}, u32[]{:S(2)}) collective-permute-start(bf16[3,2,64,512]{3,2,1,0:T(8,128)(2,1)} %collective-permute-done.4), channel_id=1, source_target_pairs={{0,192},{64,0},{128,64},{192,128},{256,448},{320,256},{384,320},{4... | collective-permute-start | bytes 1179656 | tf_op jit(solution)/shard_map/ppermute | solution.py:146
  30.4 2.0 %collective-permute-start.9 = (bf16[3,2,64,512]{3,2,1,0:T(8,128)(2,1)}, bf16[3,2,64,512]{3,2,1,0:T(8,128)(2,1)}, u32[]{:S(2)}, u32[]{:S(2)}) collective-permute-start(bf16[3,2,64,512]{3,2,1,0:T(8,128)(2,1)} %collective-permute-done.3), channel_id=1, source_target_pairs={{0,256},{64,320},{128,384},{192,448},{256,0},{320,64},{384,128},{4... | collective-permute-start | bytes 1179656 | tf_op jit(solution)/shard_map/ppermute | solution.py:146
  32.8 1.0 bitcast_dynamic-update-slice_fusion.6
  33.9 1.5 copy-done.1
  35.5 1.9 %slice_bitcast_fusion.4 = (bf16[1,256,3,2,512]{4,1,3,0,2:T(8,128)(2,1)}, bf16[1,256,3,2,512]{4,1,3,0,2:T(8,128)(2,1)}) fusion(bf16[256,4,2,512]{3,0,2,1:T(8,128)(2,1)S(1)} %copy.87, bf16[256,3,1,512]{3,0,2,1:T(8,128)(2,1)S(1)} %get-tuple-element.26, bf16[256,3,1,512]{3,0,2,1:T(8,128)(2,1)S(1)} %get-tuple-element.25), kind=kLoop, calls=%fused_computation.14 | loop fusion | flops 786432 | bytes 6291456 | tf_op jit(solution)/shard_map/stack | solution.py:177
  39.1 15.4 %all-to-all-start.1 = ((bf16[16,4,1,2,8,256]{5,4,3,1,2,0:T(8,128)(2,1)}), bf16[16,4,1,2,8,256]{5,4,3,1,2,0:T(8,128)(2,1)}, u32[]{:S(2)}, u32[]{:S(2)}) async-start(bf16[16,4,1,2,8,256]{5,4,3,1,2,0:T(8,128)(2,1)} %bitcast.162), calls=%async_computation.1 | async-start | bytes 1048576 | tf_op jit(solution)/shard_map/all_to_all | solution.py:114
  54.5 1.0 bitcast_dynamic-update-slice_fusion.5
  55.6 1.2 bitcast_dynamic-update-slice_fusion.4
  61.0 1.8 fusion.7
  62.9 1.3 copy.91
  64.2 16.5 %all-to-all-done.1 = bf16[16,4,1,2,8,256]{5,4,3,1,2,0:T(8,128)(2,1)} async-done(((bf16[16,4,1,2,8,256]{5,4,3,1,2,0:T(8,128)(2,1)}), bf16[16,4,1,2,8,256]{5,4,3,1,2,0:T(8,128)(2,1)}, u32[]{:S(2)}, u32[]{:S(2)}) %all-to-all-start.1) | async-done | bytes 524320 | tf_op jit(solution)/shard_map/all_to_all | solution.py:114
  80.7 10.9 %all-to-all-start.2 = ((bf16[64,3,2,8,256]{4,3,2,1,0:T(8,128)(2,1)}), bf16[64,3,2,8,256]{4,3,2,1,0:T(8,128)(2,1)}, u32[]{:S(2)}, u32[]{:S(2)}) async-start(bf16[64,3,2,8,256]{4,3,2,1,0:T(8,128)(2,1)} %copy.91), calls=%async_computation.2 | async-start | bytes 3145728 | tf_op jit(solution)/shard_map/all_to_all | solution.py:108
  91.7 4.6 %multiply_convert_fusion.1 = (bf16[64,4,1,1024]{3,0,1,2:T(8,128)(2,1)S(1)}, bf16[64,4,1,1024]{3,0,1,2:T(8,128)(2,1)S(1)}) fusion(f32[1024]{0:T(1024)S(1)} %broadcast_multiply_fusion, s32[64,4]{0,1:T(4,128)S(1)} %add_add_fusion), kind=kLoop, calls=%fused_computation.26 | loop fusion | flops 4980736 | bytes 1053696 | tf_op jit(solution)/shard_map/convert
  96.4 1.1 dynamic-slice_bitcast_fusion.3
  97.6 2.0 %collective-permute-start.2 = (bf16[16,1,2,8,256]{4,3,2,0,1:T(8,128)(2,1)S(1)}, bf16[16,1,2,8,256]{4,3,2,0,1:T(8,128)(2,1)S(1)}, u32[]{:S(2)}, u32[]{:S(2)}) collective-permute-start(bf16[16,1,2,8,256]{4,3,2,0,1:T(8,128)(2,1)S(1)} %get-tuple-element.32), channel_id=1, source_target_pairs={{0,3},{1,2},{2,1},{3,0},{4,7},{5,6},{6,5},{7,4},{8,11},{9,10},{10,... | collective-permute-start | bytes 393224 | tf_op jit(solution)/shard_map/ppermute | solution.py:136
  99.6 5.0 %collective-permute-start.1 = (bf16[16,1,2,8,256]{4,3,2,0,1:T(8,128)(2,1)S(1)}, bf16[16,1,2,8,256]{4,3,2,0,1:T(8,128)(2,1)S(1)}, u32[]{:S(2)}, u32[]{:S(2)}) collective-permute-start(bf16[16,1,2,8,256]{4,3,2,0,1:T(8,128)(2,1)S(1)} %get-tuple-element.30), channel_id=1, source_target_pairs={{0,2},{1,3},{2,0},{3,1},{4,6},{5,7},{6,4},{7,5},{8,10},{9,11},{10,... | collective-permute-start | bytes 393224 | tf_op jit(solution)/shard_map/ppermute | solution.py:136
  104.7 2.2 %collective-permute-start = (bf16[16,1,2,8,256]{4,3,2,0,1:T(8,128)(2,1)S(1)}, bf16[16,1,2,8,256]{4,3,2,0,1:T(8,128)(2,1)S(1)}, u32[]{:S(2)}, u32[]{:S(2)}) collective-permute-start(bf16[16,1,2,8,256]{4,3,2,0,1:T(8,128)(2,1)S(1)} %get-tuple-element.31), channel_id=1, source_target_pairs={{0,1},{1,0},{2,3},{3,2},{4,5},{5,4},{6,7},{7,6},{8,9},{9,8},{10,11... | collective-permute-start | bytes 393224 | tf_op jit(solution)/shard_map/ppermute | solution.py:136
  108.4 2.8 %collective-permute-done.1 = bf16[16,1,2,8,256]{4,3,2,0,1:T(8,128)(2,1)S(1)} collective-permute-done((bf16[16,1,2,8,256]{4,3,2,0,1:T(8,128)(2,1)S(1)}, bf16[16,1,2,8,256]{4,3,2,0,1:T(8,128)(2,1)S(1)}, u32[]{:S(2)}, u32[]{:S(2)}) %collective-permute-start.1) | collective-permute-done | bytes 131104 | tf_op jit(solution)/shard_map/ppermute | solution.py:136
  111.8 1.3 convolution_bitcast_fusion.1
  114.8 55.2 %all-to-all-done.2 = bf16[64,3,2,8,256]{4,3,2,1,0:T(8,128)(2,1)} async-done(((bf16[64,3,2,8,256]{4,3,2,1,0:T(8,128)(2,1)}), bf16[64,3,2,8,256]{4,3,2,1,0:T(8,128)(2,1)}, u32[]{:S(2)}, u32[]{:S(2)}) %all-to-all-start.2) | async-done | bytes 1572896 | tf_op jit(solution)/shard_map/all_to_all | solution.py:108
  170.1 3.9 %convolution_bitcast_fusion.frames_ref = f32[8,256,1024]{2,1,0:T(8,128)S(1)} fusion(bf16[64,3,2,8,256]{4,3,2,1,0:T(8,128)(2,1)} %all-to-all-done.2, bf16[64,4,1,1024]{3,0,1,2:T(8,128)(2,1)S(1)} %get-tuple-element.41, bf16[64,4,1,1024]{3,0,1,2:T(8,128)(2,1)S(1)} %get-tuple-element.40), kind=kOutput, calls=%fused_computation | convolution fusion | flops 1611005952 | bytes 11010048 | tf_op jit(solution)/shard_map/skcbf,skcm->bfm/dot_general | solution.py:228
  174.1 1.9 %collective-permute-start.10 = (f32[48,128]{1,0:T(8,128)S(1)}, f32[48,128]{1,0:T(8,128)S(1)}, u32[]{:S(2)}, u32[]{:S(2)}) collective-permute-start(f32[48,128]{1,0:T(8,128)S(1)} %bitcast.173), channel_id=1, source_target_pairs={{0,64},{64,128},{128,192},{192,256},{256,320},{320,384},{384,448},... | collective-permute-start | bytes 73736 | tf_op jit(solution)/shard_map/ppermute | solution.py:23
  176.0 2.1 %overlap.1 = f32[4096,128]{1,0:T(8,128)} custom-call(f32[8,256,1024]{2,1,0:T(8,128)S(1)} %convolution_bitcast_fusion.frames_ref, f32[8,256,256]{2,1,0:T(8,128)S(1)} %slice.116.base_ref), custom_call_target="tpu_custom_call" | custom-call | flops 2097152 | bytes 12582912 | tf_op jit(solution)/shard_map/overlap/pallas_call | solution.py:91
  178.2 3.7 %collective-permute-done.10 = f32[48,128]{1,0:T(8,128)S(1)} collective-permute-done((f32[48,128]{1,0:T(8,128)S(1)}, f32[48,128]{1,0:T(8,128)S(1)}, u32[]{:S(2)}, u32[]{:S(2)}) %collective-permute-start.10) | collective-permute-done | bytes 24608 | tf_op jit(solution)/shard_map/ppermute | solution.py:23
  181.9 1.4 fusion.23
  (55 shorter events, 13.1 us)
Async XLA Ops:
  1.0 21.6 %collective-permute-start.4 = (bf16[3,2,64,512]{3,2,1,0:T(8,128)(2,1)S(1)}, bf16[3,2,64,512]{3,2,1,0:T(8,128)(2,1)}, u32[]{:S(2)}, u32[]{:S(2)}) collective-permute-start(bf16[3,2,64,512]{3,2,1,0:T(8,128)(2,1)S(1)} %slice.117), channel_id=1, source_target_pairs={{0,256},{64,320},{128,384},{192,448},{256,0},{320,64},{384,128},{4... | collective-permute-start | bytes 1179656 | tf_op jit(solution)/shard_map/ppermute | solution.py:146
  3.7 26.7 %collective-permute-start.3 = (bf16[3,2,64,512]{3,2,1,0:T(8,128)(2,1)S(1)}, bf16[3,2,64,512]{3,2,1,0:T(8,128)(2,1)}, u32[]{:S(2)}, u32[]{:S(2)}) collective-permute-start(bf16[3,2,64,512]{3,2,1,0:T(8,128)(2,1)S(1)} %slice.117), channel_id=1, source_target_pairs={{0,128},{64,192},{128,0},{192,64},{256,384},{320,448},{384,256},{4... | collective-permute-start | bytes 1179656 | tf_op jit(solution)/shard_map/ppermute | solution.py:146
  9.5 20.2 %copy-start = (bf16[256,4,2,512]{3,2,1,0:T(2,128)(2,1)S(1)}, bf16[256,4,2,512]{3,2,1,0:T(2,128)(2,1)}, u32[]{:S(2)}) copy-start(bf16[256,4,2,512]{3,2,1,0:T(2,128)(2,1)} %param.3) | copy-start | bytes 6291460
  10.7 26.7 %all-to-all-start = ((bf16[8,1,2,64,512]{4,3,2,1,0:T(8,128)(2,1)}), bf16[8,1,2,64,512]{4,3,2,1,0:T(8,128)(2,1)S(1)}, u32[]{:S(2)}, u32[]{:S(2)}) async-start(bf16[8,1,2,64,512]{4,3,2,1,0:T(8,128)(2,1)} %broadcast_in_dim.39), calls=%async_computation | async-start | bytes 2097152 | tf_op jit(solution)/shard_map/all_to_all | solution.py:108
  15.4 41.4 %collective-permute-start.6 = (bf16[3,2,64,512]{3,2,1,0:T(8,128)(2,1)S(1)}, bf16[3,2,64,512]{3,2,1,0:T(8,128)(2,1)}, u32[]{:S(2)}, u32[]{:S(2)}) collective-permute-start(bf16[3,2,64,512]{3,2,1,0:T(8,128)(2,1)S(1)} %slice.117), channel_id=1, source_target_pairs={{0,64},{64,128},{128,192},{192,0},{256,320},{320,384},{384,448},{4... | collective-permute-start | bytes 1179656 | tf_op jit(solution)/shard_map/ppermute | solution.py:146
  18.8 39.0 %collective-permute-start.7 = (bf16[3,2,64,512]{3,2,1,0:T(8,128)(2,1)S(1)}, bf16[3,2,64,512]{3,2,1,0:T(8,128)(2,1)}, u32[]{:S(2)}, u32[]{:S(2)}) collective-permute-start(bf16[3,2,64,512]{3,2,1,0:T(8,128)(2,1)S(1)} %slice.117), channel_id=1, source_target_pairs={{0,192},{64,0},{128,64},{192,128},{256,448},{320,256},{384,320},{4... | collective-permute-start | bytes 1179656 | tf_op jit(solution)/shard_map/ppermute | solution.py:146
  22.6 33.0 %collective-permute-start.5 = (bf16[3,2,64,512]{3,2,1,0:T(8,128)(2,1)}, bf16[3,2,64,512]{3,2,1,0:T(8,128)(2,1)}, u32[]{:S(2)}, u32[]{:S(2)}) collective-permute-start(bf16[3,2,64,512]{3,2,1,0:T(8,128)(2,1)} %collective-permute-done.4), channel_id=1, source_target_pairs={{0,64},{64,128},{128,192},{192,0},{256,320},{320,384},{384,448},{4... | collective-permute-start | bytes 1179656 | tf_op jit(solution)/shard_map/ppermute | solution.py:146
  24.8 34.1 %collective-permute-start.8 = (bf16[3,2,64,512]{3,2,1,0:T(8,128)(2,1)}, bf16[3,2,64,512]{3,2,1,0:T(8,128)(2,1)}, u32[]{:S(2)}, u32[]{:S(2)}) collective-permute-start(bf16[3,2,64,512]{3,2,1,0:T(8,128)(2,1)} %collective-permute-done.4), channel_id=1, source_target_pairs={{0,192},{64,0},{128,64},{192,128},{256,448},{320,256},{384,320},{4... | collective-permute-start | bytes 1179656 | tf_op jit(solution)/shard_map/ppermute | solution.py:146
  30.4 29.5 %collective-permute-start.9 = (bf16[3,2,64,512]{3,2,1,0:T(8,128)(2,1)}, bf16[3,2,64,512]{3,2,1,0:T(8,128)(2,1)}, u32[]{:S(2)}, u32[]{:S(2)}) collective-permute-start(bf16[3,2,64,512]{3,2,1,0:T(8,128)(2,1)} %collective-permute-done.3), channel_id=1, source_target_pairs={{0,256},{64,320},{128,384},{192,448},{256,0},{320,64},{384,128},{4... | collective-permute-start | bytes 1179656 | tf_op jit(solution)/shard_map/ppermute | solution.py:146
  33.8 1.6 copy-start.1
  35.5 1.9 %slice-start = ((bf16[256,4,2,512]{3,2,1,0:T(2,128)(2,1)}), bf16[256,1,2,512]{3,2,1,0:T(2,128)(2,1)S(1)}, s32[]{:S(2)}) async-start(bf16[256,4,2,512]{3,2,1,0:T(2,128)(2,1)} %param.3), calls=%async_computation.3 | async-start | bytes 1048576 | tf_op jit(solution)/shard_map/slice | solution.py:210
  38.1 16.4 %copy-start.2 = (bf16[8,3,2,64,512]{4,3,2,0,1:T(8,128)(2,1)S(1)}, bf16[8,3,2,64,512]{4,3,2,0,1:T(8,128)(2,1)}, u32[]{:S(2)}) copy-start(bf16[8,3,2,64,512]{4,3,2,0,1:T(8,128)(2,1)} %copy-done.1) | copy-start | bytes 9437188
  39.1 41.5 %all-to-all-start.1 = ((bf16[16,4,1,2,8,256]{5,4,3,1,2,0:T(8,128)(2,1)}), bf16[16,4,1,2,8,256]{5,4,3,1,2,0:T(8,128)(2,1)}, u32[]{:S(2)}, u32[]{:S(2)}) async-start(bf16[16,4,1,2,8,256]{5,4,3,1,2,0:T(8,128)(2,1)} %bitcast.162), calls=%async_computation.1 | async-start | bytes 1048576 | tf_op jit(solution)/shard_map/all_to_all | solution.py:114
  55.6 5.4 %copy-start.3 = (bf16[1,256,3,2,512]{4,1,3,0,2:T(8,128)(2,1)S(1)}, bf16[1,256,3,2,512]{4,1,3,0,2:T(8,128)(2,1)}, u32[]{:S(2)}) copy-start(bf16[1,256,3,2,512]{4,1,3,0,2:T(8,128)(2,1)} %get-tuple-element.42) | copy-start | bytes 4718596
  55.6 5.4 %copy-start.4 = (bf16[1,256,3,2,512]{4,1,3,0,2:T(8,128)(2,1)S(1)}, bf16[1,256,3,2,512]{4,1,3,0,2:T(8,128)(2,1)}, u32[]{:S(2)}) copy-start(bf16[1,256,3,2,512]{4,1,3,0,2:T(8,128)(2,1)} %get-tuple-element.43) | copy-start | bytes 4718596
  64.2 27.4 %copy-start.5 = (f32[1024]{0:T(1024)S(1)}, f32[1024]{0:T(1024)}, u32[]{:S(2)}) copy-start(f32[1024]{0:T(1024)} %param.5) | copy-start | bytes 12292
  80.7 89.4 %all-to-all-start.2 = ((bf16[64,3,2,8,256]{4,3,2,1,0:T(8,128)(2,1)}), bf16[64,3,2,8,256]{4,3,2,1,0:T(8,128)(2,1)}, u32[]{:S(2)}, u32[]{:S(2)}) async-start(bf16[64,3,2,8,256]{4,3,2,1,0:T(8,128)(2,1)} %copy.91), calls=%async_computation.2 | async-start | bytes 3145728 | tf_op jit(solution)/shard_map/all_to_all | solution.py:108
  97.6 10.8 %collective-permute-start.2 = (bf16[16,1,2,8,256]{4,3,2,0,1:T(8,128)(2,1)S(1)}, bf16[16,1,2,8,256]{4,3,2,0,1:T(8,128)(2,1)S(1)}, u32[]{:S(2)}, u32[]{:S(2)}) collective-permute-start(bf16[16,1,2,8,256]{4,3,2,0,1:T(8,128)(2,1)S(1)} %get-tuple-element.32), channel_id=1, source_target_pairs={{0,3},{1,2},{2,1},{3,0},{4,7},{5,6},{6,5},{7,4},{8,11},{9,10},{10,... | collective-permute-start | bytes 393224 | tf_op jit(solution)/shard_map/ppermute | solution.py:136
  99.6 11.6 %collective-permute-start.1 = (bf16[16,1,2,8,256]{4,3,2,0,1:T(8,128)(2,1)S(1)}, bf16[16,1,2,8,256]{4,3,2,0,1:T(8,128)(2,1)S(1)}, u32[]{:S(2)}, u32[]{:S(2)}) collective-permute-start(bf16[16,1,2,8,256]{4,3,2,0,1:T(8,128)(2,1)S(1)} %get-tuple-element.30), channel_id=1, source_target_pairs={{0,2},{1,3},{2,0},{3,1},{4,6},{5,7},{6,4},{7,5},{8,10},{9,11},{10,... | collective-permute-start | bytes 393224 | tf_op jit(solution)/shard_map/ppermute | solution.py:136
  104.7 6.5 %collective-permute-start = (bf16[16,1,2,8,256]{4,3,2,0,1:T(8,128)(2,1)S(1)}, bf16[16,1,2,8,256]{4,3,2,0,1:T(8,128)(2,1)S(1)}, u32[]{:S(2)}, u32[]{:S(2)}) collective-permute-start(bf16[16,1,2,8,256]{4,3,2,0,1:T(8,128)(2,1)S(1)} %get-tuple-element.31), channel_id=1, source_target_pairs={{0,1},{1,0},{2,3},{3,2},{4,5},{5,4},{6,7},{7,6},{8,9},{9,8},{10,11... | collective-permute-start | bytes 393224 | tf_op jit(solution)/shard_map/ppermute | solution.py:136
  174.1 7.8 %collective-permute-start.10 = (f32[48,128]{1,0:T(8,128)S(1)}, f32[48,128]{1,0:T(8,128)S(1)}, u32[]{:S(2)}, u32[]{:S(2)}) collective-permute-start(f32[48,128]{1,0:T(8,128)S(1)} %bitcast.173), channel_id=1, source_target_pairs={{0,64},{64,128},{128,192},{192,256},{256,320},{320,384},{384,448},... | collective-permute-start | bytes 73736 | tf_op jit(solution)/shard_map/ppermute | solution.py:23

commit v6 on v5

--- a/solution.py
+++ b/solution.py
@@ -148,16 +148,17 @@
 
 def own_row(block):
     across = across_tm(block, 0, 1)
-    left, right = across_tm(block, 1, 0), across_tm(block, -1, 0)
+    left = across_tm(block, 1, 0)
     far = across_tm(block, 2, 0)
-    return left, right, across, far
-
-
-def whole_table(block, left, right, across, far):
+    return left, across, far
+
+
+def whole_table(block, left, across, far):
     across_left = across_tm(across, 1, 0)
     across_right = across_tm(across, -1, 0)
     far, block = lax.optimization_barrier((far, block))
     across_far = across_tm(far, 0, 1)
+    right = across_tm(block, -1, 0)
     size = lax.axis_size("tm")
     ring = size // 2
     me = lax.axis_index("tm")
@@ -206,13 +207,13 @@
     size = lax.axis_size("tm")
     head = blocks[:HEAD]
     head = exchanged(jnp.broadcast_to(head[None], (size,) + head.shape), "tm")
-    left, right, across, far = own_row(blocks[HEAD:])
+    left, across, far = own_row(blocks[HEAD:])
     message = beam_form_of_pairs(samples[:, :HEAD], head)
     head_spectra = along_z(in_planes(message))
     samples, across, block, _ = lax.optimization_barrier(
         (samples, across, blocks[HEAD:], message)
     )
-    rest = whole_table(block, left, right, across, far)
+    rest = whole_table(block, left, across, far)
     rest_message = beam_form(with_quadrature(samples[:, HEAD:]), rest)
     rest_spectra = exchanged(rest_message, "band")
     head_spectra = within_plane(head_spectra).reshape(message.shape)

time: 184 us -> 183 us (level)
  transfers between devices with their start and end apart: 14 -> 14, of which waited for: 4 -> 4; matrix products, arithmetic and copies ran while one was open for 15% -> 16% of each run, Pallas kernels for 1% -> 1%
where the time goes in v6:
time: 183 us; the launch traced here: 182 us
  waiting for transfers between devices  76.6 us (42%)
  starting transfers between devices  66.3 us (36%)
  local copies, waits for them, and re-layouts  18.1 us (10%)
  other arithmetic  10.4 us (6%)
  matrix products  7.74 us (4%)
  Pallas kernels  2.15 us (1%)
    all_to_all x2, waiting for transfers between devices, exchanged(): return lax.all_to_all(block, axis, split_axis=0, concat_axis=0, tiled=True)  55.2 us
    ppermute x7, starting transfers between devices, across_tm(): return lax.ppermute(array, 'tm', route)  22.5 us
    all_to_all x1, waiting for transfers between devices, along_z(): lax.all_to_all(block, 'band', split_axis=0, concat_axis=0, tiled=True, ax...  16.5 us
    all_to_all x2, starting transfers between devices, exchanged(): return lax.all_to_all(block, axis, split_axis=0, concat_axis=0, tiled=True)  15.7 us
    all_to_all x1, starting transfers between devices, along_z(): lax.all_to_all(block, 'band', split_axis=0, concat_axis=0, tiled=True, ax...  15.4 us
    ppermute x3, starting transfers between devices, within_plane(): pieces[step] = lax.ppermute(pieces[step], 'band', route)  9.27 us
    dynamic_update_slice x7, local copies, waits for them, and re-layouts, whole_table(): lax.dynamic_update_slice(table, piece[None], (at,) + (0,) * block.ndim)  7.35 us
    dot_general x2, matrix products, synthesize(): jnp.einsum('skcbf,skcm->bfm', spectra, part, preferred_element_type=jnp.f...  5.16 us
  transfers between devices with their start and end apart: 14, of which 4 were waited for; matrix products, arithmetic and copies ran while one was open for 16% of the time, Pallas kernels for 1%

profile of v6, /device:TPU:24, one launch (start us, length us, event | category | flops | bytes accessed | tf_op | source)
XLA Modules:
  0.0 182.1 jit_solution(11840907774785410989)
XLA Ops:
  1.0 2.7 %collective-permute-start.4 = (bf16[3,2,64,512]{3,2,1,0:T(8,128)(2,1)S(1)}, bf16[3,2,64,512]{3,2,1,0:T(8,128)(2,1)}, u32[]{:S(2)}, u32[]{:S(2)}) collective-permute-start(bf16[3,2,64,512]{3,2,1,0:T(8,128)(2,1)S(1)} %slice.117), channel_id=1, source_target_pairs={{0,256},{64,320},{128,384},{192,448},{256,0},{320,64},{384,128},{4... | collective-permute-start | bytes 1179656 | tf_op jit(solution)/shard_map/ppermute | solution.py:146
  3.7 4.9 %collective-permute-start.3 = (bf16[3,2,64,512]{3,2,1,0:T(8,128)(2,1)S(1)}, bf16[3,2,64,512]{3,2,1,0:T(8,128)(2,1)}, u32[]{:S(2)}, u32[]{:S(2)}) collective-permute-start(bf16[3,2,64,512]{3,2,1,0:T(8,128)(2,1)S(1)} %slice.117), channel_id=1, source_target_pairs={{0,128},{64,192},{128,0},{192,64},{256,384},{320,448},{384,256},{4... | collective-permute-start | bytes 1179656 | tf_op jit(solution)/shard_map/ppermute | solution.py:146
  9.6 1.1 broadcast_in_dim.39
  10.7 4.8 %all-to-all-start = ((bf16[8,1,2,64,512]{4,3,2,1,0:T(8,128)(2,1)}), bf16[8,1,2,64,512]{4,3,2,1,0:T(8,128)(2,1)S(1)}, u32[]{:S(2)}, u32[]{:S(2)}) async-start(bf16[8,1,2,64,512]{4,3,2,1,0:T(8,128)(2,1)} %broadcast_in_dim.39), calls=%async_computation | async-start | bytes 2097152 | tf_op jit(solution)/shard_map/all_to_all | solution.py:108
  15.4 3.4 %collective-permute-start.6 = (bf16[3,2,64,512]{3,2,1,0:T(8,128)(2,1)S(1)}, bf16[3,2,64,512]{3,2,1,0:T(8,128)(2,1)}, u32[]{:S(2)}, u32[]{:S(2)}) collective-permute-start(bf16[3,2,64,512]{3,2,1,0:T(8,128)(2,1)S(1)} %slice.117), channel_id=1, source_target_pairs={{0,64},{64,128},{128,192},{192,0},{256,320},{320,384},{384,448},{4... | collective-permute-start | bytes 1179656 | tf_op jit(solution)/shard_map/ppermute | solution.py:146
  18.9 3.4 %collective-permute-start.5 = (bf16[3,2,64,512]{3,2,1,0:T(8,128)(2,1)}, bf16[3,2,64,512]{3,2,1,0:T(8,128)(2,1)}, u32[]{:S(2)}, u32[]{:S(2)}) collective-permute-start(bf16[3,2,64,512]{3,2,1,0:T(8,128)(2,1)} %collective-permute-done.4), channel_id=1, source_target_pairs={{0,64},{64,128},{128,192},{192,0},{256,320},{320,384},{384,448},{4... | collective-permute-start | bytes 1179656 | tf_op jit(solution)/shard_map/ppermute | solution.py:146
  22.3 3.7 %collective-permute-start.8 = (bf16[3,2,64,512]{3,2,1,0:T(8,128)(2,1)}, bf16[3,2,64,512]{3,2,1,0:T(8,128)(2,1)}, u32[]{:S(2)}, u32[]{:S(2)}) collective-permute-start(bf16[3,2,64,512]{3,2,1,0:T(8,128)(2,1)} %collective-permute-done.4), channel_id=1, source_target_pairs={{0,192},{64,0},{128,64},{192,128},{256,448},{320,256},{384,320},{4... | collective-permute-start | bytes 1179656 | tf_op jit(solution)/shard_map/ppermute | solution.py:146
  26.7 2.5 %collective-permute-start.7 = (bf16[3,2,64,512]{3,2,1,0:T(8,128)(2,1)S(1)}, bf16[3,2,64,512]{3,2,1,0:T(8,128)(2,1)}, u32[]{:S(2)}, u32[]{:S(2)}) collective-permute-start(bf16[3,2,64,512]{3,2,1,0:T(8,128)(2,1)S(1)} %slice.117), channel_id=1, source_target_pairs={{0,192},{64,0},{128,64},{192,128},{256,448},{320,256},{384,320},{4... | collective-permute-start | bytes 1179656 | tf_op jit(solution)/shard_map/ppermute | solution.py:146
  29.2 2.0 %collective-permute-start.9 = (bf16[3,2,64,512]{3,2,1,0:T(8,128)(2,1)}, bf16[3,2,64,512]{3,2,1,0:T(8,128)(2,1)}, u32[]{:S(2)}, u32[]{:S(2)}) collective-permute-start(bf16[3,2,64,512]{3,2,1,0:T(8,128)(2,1)} %collective-permute-done.3), channel_id=1, source_target_pairs={{0,256},{64,320},{128,384},{192,448},{256,0},{320,64},{384,128},{4... | collective-permute-start | bytes 1179656 | tf_op jit(solution)/shard_map/ppermute | solution.py:146
  31.6 1.0 bitcast_dynamic-update-slice_fusion.6
  32.7 1.5 copy-done.1
  34.2 1.9 %slice_bitcast_fusion.4 = (bf16[1,256,3,2,512]{4,1,3,0,2:T(8,128)(2,1)}, bf16[1,256,3,2,512]{4,1,3,0,2:T(8,128)(2,1)}) fusion(bf16[256,4,2,512]{3,0,2,1:T(8,128)(2,1)S(1)} %copy.87, bf16[256,3,1,512]{3,0,2,1:T(8,128)(2,1)S(1)} %get-tuple-element.26, bf16[256,3,1,512]{3,0,2,1:T(8,128)(2,1)S(1)} %get-tuple-element.25), kind=kLoop, calls=%fused_computation.14 | loop fusion | flops 786432 | bytes 6291456 | tf_op jit(solution)/shard_map/stack | solution.py:178
  37.9 15.4 %all-to-all-start.1 = ((bf16[16,4,1,2,8,256]{5,4,3,1,2,0:T(8,128)(2,1)}), bf16[16,4,1,2,8,256]{5,4,3,1,2,0:T(8,128)(2,1)}, u32[]{:S(2)}, u32[]{:S(2)}) async-start(bf16[16,4,1,2,8,256]{5,4,3,1,2,0:T(8,128)(2,1)} %bitcast.162), calls=%async_computation.1 | async-start | bytes 1048576 | tf_op jit(solution)/shard_map/all_to_all | solution.py:114
  53.3 1.0 bitcast_dynamic-update-slice_fusion.5
  54.4 1.2 bitcast_dynamic-update-slice_fusion.4
  59.8 1.8 %fusion.7 = bf16[8,64,3,2,256]{4,1,3,0,2:T(8,128)(2,1)S(1)} fusion(bf16[1,256,3,2,512]{4,1,3,0,2:T(8,128)(2,1)S(1)} %copy-done.4, bf16[1,256,3,2,512]{4,1,3,0,2:T(8,128)(2,1)S(1)} %copy-done.3, bf16[8,3,2,64,512]{4,3,2,0,1:T(8,128)(2,1)S(1)} %bitcast_dynamic-update-slice_fusion), kind=kOutput, calls=%fused_computation.20 | convolution fusion | flops 1617690624 | bytes 7864320 | tf_op jit(solution)/shard_map/pfkce,tkcbe->tbkpf/dot_general | solution.py:198
  61.7 1.3 copy.91
  63.0 16.5 %all-to-all-done.1 = bf16[16,4,1,2,8,256]{5,4,3,1,2,0:T(8,128)(2,1)} async-done(((bf16[16,4,1,2,8,256]{5,4,3,1,2,0:T(8,128)(2,1)}), bf16[16,4,1,2,8,256]{5,4,3,1,2,0:T(8,128)(2,1)}, u32[]{:S(2)}, u32[]{:S(2)}) %all-to-all-start.1) | async-done | bytes 524320 | tf_op jit(solution)/shard_map/all_to_all | solution.py:114
  79.5 10.9 %all-to-all-start.2 = ((bf16[64,3,2,8,256]{4,3,2,1,0:T(8,128)(2,1)}), bf16[64,3,2,8,256]{4,3,2,1,0:T(8,128)(2,1)}, u32[]{:S(2)}, u32[]{:S(2)}) async-start(bf16[64,3,2,8,256]{4,3,2,1,0:T(8,128)(2,1)} %copy.91), calls=%async_computation.2 | async-start | bytes 3145728 | tf_op jit(solution)/shard_map/all_to_all | solution.py:108
  90.5 4.6 %multiply_convert_fusion.1 = (bf16[64,4,1,1024]{3,0,1,2:T(8,128)(2,1)S(1)}, bf16[64,4,1,1024]{3,0,1,2:T(8,128)(2,1)S(1)}) fusion(f32[1024]{0:T(1024)S(1)} %broadcast_multiply_fusion, s32[64,4]{0,1:T(4,128)S(1)} %add_add_fusion), kind=kLoop, calls=%fused_computation.26 | loop fusion | flops 4980736 | bytes 1053696 | tf_op jit(solution)/shard_map/convert
  95.2 1.1 dynamic-slice_bitcast_fusion.3
  96.4 2.0 %collective-permute-start.2 = (bf16[16,1,2,8,256]{4,3,2,0,1:T(8,128)(2,1)S(1)}, bf16[16,1,2,8,256]{4,3,2,0,1:T(8,128)(2,1)S(1)}, u32[]{:S(2)}, u32[]{:S(2)}) collective-permute-start(bf16[16,1,2,8,256]{4,3,2,0,1:T(8,128)(2,1)S(1)} %get-tuple-element.32), channel_id=1, source_target_pairs={{0,3},{1,2},{2,1},{3,0},{4,7},{5,6},{6,5},{7,4},{8,11},{9,10},{10,... | collective-permute-start | bytes 393224 | tf_op jit(solution)/shard_map/ppermute | solution.py:136
  98.4 5.0 %collective-permute-start.1 = (bf16[16,1,2,8,256]{4,3,2,0,1:T(8,128)(2,1)S(1)}, bf16[16,1,2,8,256]{4,3,2,0,1:T(8,128)(2,1)S(1)}, u32[]{:S(2)}, u32[]{:S(2)}) collective-permute-start(bf16[16,1,2,8,256]{4,3,2,0,1:T(8,128)(2,1)S(1)} %get-tuple-element.30), channel_id=1, source_target_pairs={{0,2},{1,3},{2,0},{3,1},{4,6},{5,7},{6,4},{7,5},{8,10},{9,11},{10,... | collective-permute-start | bytes 393224 | tf_op jit(solution)/shard_map/ppermute | solution.py:136
  103.5 2.2 %collective-permute-start = (bf16[16,1,2,8,256]{4,3,2,0,1:T(8,128)(2,1)S(1)}, bf16[16,1,2,8,256]{4,3,2,0,1:T(8,128)(2,1)S(1)}, u32[]{:S(2)}, u32[]{:S(2)}) collective-permute-start(bf16[16,1,2,8,256]{4,3,2,0,1:T(8,128)(2,1)S(1)} %get-tuple-element.31), channel_id=1, source_target_pairs={{0,1},{1,0},{2,3},{3,2},{4,5},{5,4},{6,7},{7,6},{8,9},{9,8},{10,11... | collective-permute-start | bytes 393224 | tf_op jit(solution)/shard_map/ppermute | solution.py:136
  107.2 2.8 %collective-permute-done.1 = bf16[16,1,2,8,256]{4,3,2,0,1:T(8,128)(2,1)S(1)} collective-permute-done((bf16[16,1,2,8,256]{4,3,2,0,1:T(8,128)(2,1)S(1)}, bf16[16,1,2,8,256]{4,3,2,0,1:T(8,128)(2,1)S(1)}, u32[]{:S(2)}, u32[]{:S(2)}) %collective-permute-start.1) | collective-permute-done | bytes 131104 | tf_op jit(solution)/shard_map/ppermute | solution.py:136
  110.6 1.3 convolution_bitcast_fusion.1
  113.6 55.2 %all-to-all-done.2 = bf16[64,3,2,8,256]{4,3,2,1,0:T(8,128)(2,1)} async-done(((bf16[64,3,2,8,256]{4,3,2,1,0:T(8,128)(2,1)}), bf16[64,3,2,8,256]{4,3,2,1,0:T(8,128)(2,1)}, u32[]{:S(2)}, u32[]{:S(2)}) %all-to-all-start.2) | async-done | bytes 1572896 | tf_op jit(solution)/shard_map/all_to_all | solution.py:108
  168.8 3.9 %convolution_bitcast_fusion.frames_ref = f32[8,256,1024]{2,1,0:T(8,128)S(1)} fusion(bf16[64,3,2,8,256]{4,3,2,1,0:T(8,128)(2,1)} %all-to-all-done.2, bf16[64,4,1,1024]{3,0,1,2:T(8,128)(2,1)S(1)} %get-tuple-element.41, bf16[64,4,1,1024]{3,0,1,2:T(8,128)(2,1)S(1)} %get-tuple-element.40), kind=kOutput, calls=%fused_computation | convolution fusion | flops 1611005952 | bytes 11010048 | tf_op jit(solution)/shard_map/skcbf,skcm->bfm/dot_general | solution.py:229
  172.9 3.5 %collective-permute-start.10 = (f32[48,128]{1,0:T(8,128)S(1)}, f32[48,128]{1,0:T(8,128)S(1)}, u32[]{:S(2)}, u32[]{:S(2)}) collective-permute-start(f32[48,128]{1,0:T(8,128)S(1)} %bitcast.173), channel_id=1, source_target_pairs={{0,64},{64,128},{128,192},{192,256},{256,320},{320,384},{384,448},... | collective-permute-start | bytes 73736 | tf_op jit(solution)/shard_map/ppermute | solution.py:23
  176.4 2.1 %overlap.1 = f32[4096,128]{1,0:T(8,128)} custom-call(f32[8,256,1024]{2,1,0:T(8,128)S(1)} %convolution_bitcast_fusion.frames_ref, f32[8,256,256]{2,1,0:T(8,128)S(1)} %slice.116.base_ref), custom_call_target="tpu_custom_call" | custom-call | flops 2097152 | bytes 12582912 | tf_op jit(solution)/shard_map/overlap/pallas_call | solution.py:91
  178.6 2.1 %collective-permute-done.10 = f32[48,128]{1,0:T(8,128)S(1)} collective-permute-done((f32[48,128]{1,0:T(8,128)S(1)}, f32[48,128]{1,0:T(8,128)S(1)}, u32[]{:S(2)}, u32[]{:S(2)}) %collective-permute-start.10) | collective-permute-done | bytes 24608 | tf_op jit(solution)/shard_map/ppermute | solution.py:23
  180.7 1.4 fusion.23
  (55 shorter events, 13.1 us)
Async XLA Ops:
  1.0 17.9 %collective-permute-start.4 = (bf16[3,2,64,512]{3,2,1,0:T(8,128)(2,1)S(1)}, bf16[3,2,64,512]{3,2,1,0:T(8,128)(2,1)}, u32[]{:S(2)}, u32[]{:S(2)}) collective-permute-start(bf16[3,2,64,512]{3,2,1,0:T(8,128)(2,1)S(1)} %slice.117), channel_id=1, source_target_pairs={{0,256},{64,320},{128,384},{192,448},{256,0},{320,64},{384,128},{4... | collective-permute-start | bytes 1179656 | tf_op jit(solution)/shard_map/ppermute | solution.py:146
  3.7 23.0 %collective-permute-start.3 = (bf16[3,2,64,512]{3,2,1,0:T(8,128)(2,1)S(1)}, bf16[3,2,64,512]{3,2,1,0:T(8,128)(2,1)}, u32[]{:S(2)}, u32[]{:S(2)}) collective-permute-start(bf16[3,2,64,512]{3,2,1,0:T(8,128)(2,1)S(1)} %slice.117), channel_id=1, source_target_pairs={{0,128},{64,192},{128,0},{192,64},{256,384},{320,448},{384,256},{4... | collective-permute-start | bytes 1179656 | tf_op jit(solution)/shard_map/ppermute | solution.py:146
  9.5 16.5 %copy-start = (bf16[256,4,2,512]{3,2,1,0:T(2,128)(2,1)S(1)}, bf16[256,4,2,512]{3,2,1,0:T(2,128)(2,1)}, u32[]{:S(2)}) copy-start(bf16[256,4,2,512]{3,2,1,0:T(2,128)(2,1)} %param.3) | copy-start | bytes 6291460
  10.7 25.5 %all-to-all-start = ((bf16[8,1,2,64,512]{4,3,2,1,0:T(8,128)(2,1)}), bf16[8,1,2,64,512]{4,3,2,1,0:T(8,128)(2,1)S(1)}, u32[]{:S(2)}, u32[]{:S(2)}) async-start(bf16[8,1,2,64,512]{4,3,2,1,0:T(8,128)(2,1)} %broadcast_in_dim.39), calls=%async_computation | async-start | bytes 2097152 | tf_op jit(solution)/shard_map/all_to_all | solution.py:108
  15.4 40.1 %collective-permute-start.6 = (bf16[3,2,64,512]{3,2,1,0:T(8,128)(2,1)S(1)}, bf16[3,2,64,512]{3,2,1,0:T(8,128)(2,1)}, u32[]{:S(2)}, u32[]{:S(2)}) collective-permute-start(bf16[3,2,64,512]{3,2,1,0:T(8,128)(2,1)S(1)} %slice.117), channel_id=1, source_target_pairs={{0,64},{64,128},{128,192},{192,0},{256,320},{320,384},{384,448},{4... | collective-permute-start | bytes 1179656 | tf_op jit(solution)/shard_map/ppermute | solution.py:146
  18.9 35.4 %collective-permute-start.5 = (bf16[3,2,64,512]{3,2,1,0:T(8,128)(2,1)}, bf16[3,2,64,512]{3,2,1,0:T(8,128)(2,1)}, u32[]{:S(2)}, u32[]{:S(2)}) collective-permute-start(bf16[3,2,64,512]{3,2,1,0:T(8,128)(2,1)} %collective-permute-done.4), channel_id=1, source_target_pairs={{0,64},{64,128},{128,192},{192,0},{256,320},{320,384},{384,448},{4... | collective-permute-start | bytes 1179656 | tf_op jit(solution)/shard_map/ppermute | solution.py:146
  22.3 35.3 %collective-permute-start.8 = (bf16[3,2,64,512]{3,2,1,0:T(8,128)(2,1)}, bf16[3,2,64,512]{3,2,1,0:T(8,128)(2,1)}, u32[]{:S(2)}, u32[]{:S(2)}) collective-permute-start(bf16[3,2,64,512]{3,2,1,0:T(8,128)(2,1)} %collective-permute-done.4), channel_id=1, source_target_pairs={{0,192},{64,0},{128,64},{192,128},{256,448},{320,256},{384,320},{4... | collective-permute-start | bytes 1179656 | tf_op jit(solution)/shard_map/ppermute | solution.py:146
  26.7 29.9 %collective-permute-start.7 = (bf16[3,2,64,512]{3,2,1,0:T(8,128)(2,1)S(1)}, bf16[3,2,64,512]{3,2,1,0:T(8,128)(2,1)}, u32[]{:S(2)}, u32[]{:S(2)}) collective-permute-start(bf16[3,2,64,512]{3,2,1,0:T(8,128)(2,1)S(1)} %slice.117), channel_id=1, source_target_pairs={{0,192},{64,0},{128,64},{192,128},{256,448},{320,256},{384,320},{4... | collective-permute-start | bytes 1179656 | tf_op jit(solution)/shard_map/ppermute | solution.py:146
  29.2 29.5 %collective-permute-start.9 = (bf16[3,2,64,512]{3,2,1,0:T(8,128)(2,1)}, bf16[3,2,64,512]{3,2,1,0:T(8,128)(2,1)}, u32[]{:S(2)}, u32[]{:S(2)}) collective-permute-start(bf16[3,2,64,512]{3,2,1,0:T(8,128)(2,1)} %collective-permute-done.3), channel_id=1, source_target_pairs={{0,256},{64,320},{128,384},{192,448},{256,0},{320,64},{384,128},{4... | collective-permute-start | bytes 1179656 | tf_op jit(solution)/shard_map/ppermute | solution.py:146
  32.6 1.6 copy-start.1
  34.2 1.9 %slice-start = ((bf16[256,4,2,512]{3,2,1,0:T(2,128)(2,1)}), bf16[256,1,2,512]{3,2,1,0:T(2,128)(2,1)S(1)}, s32[]{:S(2)}) async-start(bf16[256,4,2,512]{3,2,1,0:T(2,128)(2,1)} %param.3), calls=%async_computation.3 | async-start | bytes 1048576 | tf_op jit(solution)/shard_map/slice | solution.py:211
  36.9 16.4 %copy-start.2 = (bf16[8,3,2,64,512]{4,3,2,0,1:T(8,128)(2,1)S(1)}, bf16[8,3,2,64,512]{4,3,2,0,1:T(8,128)(2,1)}, u32[]{:S(2)}) copy-start(bf16[8,3,2,64,512]{4,3,2,0,1:T(8,128)(2,1)} %copy-done.1) | copy-start | bytes 9437188
  37.9 41.5 %all-to-all-start.1 = ((bf16[16,4,1,2,8,256]{5,4,3,1,2,0:T(8,128)(2,1)}), bf16[16,4,1,2,8,256]{5,4,3,1,2,0:T(8,128)(2,1)}, u32[]{:S(2)}, u32[]{:S(2)}) async-start(bf16[16,4,1,2,8,256]{5,4,3,1,2,0:T(8,128)(2,1)} %bitcast.162), calls=%async_computation.1 | async-start | bytes 1048576 | tf_op jit(solution)/shard_map/all_to_all | solution.py:114
  54.4 5.4 %copy-start.3 = (bf16[1,256,3,2,512]{4,1,3,0,2:T(8,128)(2,1)S(1)}, bf16[1,256,3,2,512]{4,1,3,0,2:T(8,128)(2,1)}, u32[]{:S(2)}) copy-start(bf16[1,256,3,2,512]{4,1,3,0,2:T(8,128)(2,1)} %get-tuple-element.42) | copy-start | bytes 4718596
  54.4 5.4 %copy-start.4 = (bf16[1,256,3,2,512]{4,1,3,0,2:T(8,128)(2,1)S(1)}, bf16[1,256,3,2,512]{4,1,3,0,2:T(8,128)(2,1)}, u32[]{:S(2)}) copy-start(bf16[1,256,3,2,512]{4,1,3,0,2:T(8,128)(2,1)} %get-tuple-element.43) | copy-start | bytes 4718596
  63.0 27.4 %copy-start.5 = (f32[1024]{0:T(1024)S(1)}, f32[1024]{0:T(1024)}, u32[]{:S(2)}) copy-start(f32[1024]{0:T(1024)} %param.5) | copy-start | bytes 12292
  79.5 89.4 %all-to-all-start.2 = ((bf16[64,3,2,8,256]{4,3,2,1,0:T(8,128)(2,1)}), bf16[64,3,2,8,256]{4,3,2,1,0:T(8,128)(2,1)}, u32[]{:S(2)}, u32[]{:S(2)}) async-start(bf16[64,3,2,8,256]{4,3,2,1,0:T(8,128)(2,1)} %copy.91), calls=%async_computation.2 | async-start | bytes 3145728 | tf_op jit(solution)/shard_map/all_to_all | solution.py:108
  96.4 10.8 %collective-permute-start.2 = (bf16[16,1,2,8,256]{4,3,2,0,1:T(8,128)(2,1)S(1)}, bf16[16,1,2,8,256]{4,3,2,0,1:T(8,128)(2,1)S(1)}, u32[]{:S(2)}, u32[]{:S(2)}) collective-permute-start(bf16[16,1,2,8,256]{4,3,2,0,1:T(8,128)(2,1)S(1)} %get-tuple-element.32), channel_id=1, source_target_pairs={{0,3},{1,2},{2,1},{3,0},{4,7},{5,6},{6,5},{7,4},{8,11},{9,10},{10,... | collective-permute-start | bytes 393224 | tf_op jit(solution)/shard_map/ppermute | solution.py:136
  98.4 11.6 %collective-permute-start.1 = (bf16[16,1,2,8,256]{4,3,2,0,1:T(8,128)(2,1)S(1)}, bf16[16,1,2,8,256]{4,3,2,0,1:T(8,128)(2,1)S(1)}, u32[]{:S(2)}, u32[]{:S(2)}) collective-permute-start(bf16[16,1,2,8,256]{4,3,2,0,1:T(8,128)(2,1)S(1)} %get-tuple-element.30), channel_id=1, source_target_pairs={{0,2},{1,3},{2,0},{3,1},{4,6},{5,7},{6,4},{7,5},{8,10},{9,11},{10,... | collective-permute-start | bytes 393224 | tf_op jit(solution)/shard_map/ppermute | solution.py:136
  103.5 6.5 %collective-permute-start = (bf16[16,1,2,8,256]{4,3,2,0,1:T(8,128)(2,1)S(1)}, bf16[16,1,2,8,256]{4,3,2,0,1:T(8,128)(2,1)S(1)}, u32[]{:S(2)}, u32[]{:S(2)}) collective-permute-start(bf16[16,1,2,8,256]{4,3,2,0,1:T(8,128)(2,1)S(1)} %get-tuple-element.31), channel_id=1, source_target_pairs={{0,1},{1,0},{2,3},{3,2},{4,5},{5,4},{6,7},{7,6},{8,9},{9,8},{10,11... | collective-permute-start | bytes 393224 | tf_op jit(solution)/shard_map/ppermute | solution.py:136
  172.9 7.8 %collective-permute-start.10 = (f32[48,128]{1,0:T(8,128)S(1)}, f32[48,128]{1,0:T(8,128)S(1)}, u32[]{:S(2)}, u32[]{:S(2)}) collective-permute-start(f32[48,128]{1,0:T(8,128)S(1)} %bitcast.173), channel_id=1, source_target_pairs={{0,64},{64,128},{128,192},{192,256},{256,320},{320,384},{384,448},... | collective-permute-start | bytes 73736 | tf_op jit(solution)/shard_map/ppermute | solution.py:23
